TPU v7x, 8 devices: a whole 2x2x1 slice. The times are simulated.
8 devices in a mesh: tp: 4 (over z, y, x), dp: 2 (over core).
Axes of the slice: x: 2, y: 2, z: 1, core: 2. Of those that a mesh axis runs over, the one named last changes fastest.
Arguments:
- x: bfloat16 [16384, 5120], P(('dp', 'tp'))
- w_gate: bfloat16 [5120, 13824], P('dp', 'tp')
- w_up: bfloat16 [5120, 13824], P('dp', 'tp')
- w_down: bfloat16 [13824, 5120], P('tp', 'dp')
Outputs:
- output: bfloat16 [16384, 5120], P(('dp', 'tp'))
All inputs are finite; a program needn't handle non-finite values.
Results may differ from a plain program's by a relative error of at most 0.0131407.
Values are sent between devices in bfloat16 or wider.
A program may use at most 1 GiB of HBM per device.

v0:
```python
import jax
import jax.numpy as jnp
from jax import lax
from jax.sharding import PartitionSpec as P


def solution(mesh):
    nt = mesh.shape["tp"]
    nd = mesh.shape["dp"]

    def body(x, wg, wu, wd):
        r, d = x.shape
        dc = d // nd
        xt = lax.all_gather(x, "tp", axis=0, tiled=True)
        xc = lax.all_to_all(xt, "dp", 1, 0, tiled=True)
        pa = jnp.dot(xc, wg, preferred_element_type=jnp.float32).astype(jnp.bfloat16)
        pb = jnp.dot(xc, wu, preferred_element_type=jnp.float32).astype(jnp.bfloat16)
        a = lax.psum_scatter(pa, "dp", scatter_dimension=0, tiled=True).astype(jnp.float32)
        b = lax.psum_scatter(pb, "dp", scatter_dimension=0, tiled=True).astype(jnp.float32)
        h = (jax.nn.silu(a) * b).astype(jnp.bfloat16)
        hg = lax.all_gather(h, "dp", axis=0, tiled=True)
        po = jnp.dot(hg, wd, preferred_element_type=jnp.float32).astype(jnp.bfloat16)
        po = po.reshape(nd, nt, r, dc)
        ps = lax.psum_scatter(po, "tp", scatter_dimension=1, tiled=True)
        o = lax.all_to_all(ps.reshape(nd, r, dc), "dp", 0, 0, tiled=True)
        o = o.transpose(1, 0, 2).reshape(r, d)
        return (x.astype(jnp.float32) + o.astype(jnp.float32)).astype(jnp.bfloat16)

    return jax.shard_map(body, mesh=mesh, in_specs=(P(("dp", "tp"), None), P("dp", "tp"), P("dp", "tp"), P("tp", "dp")), out_specs=P(("dp", "tp"), None), check_vma=False)
```

profile of v0, /device:TPU:0, one launch (start us, length us, event | category | flops | bytes accessed | tf_op | source)
XLA Modules:
  0.0 3738.3 jit_solution(10642329861521961706)
XLA Ops:
  6.5 0.0 all-gather.3.cloned.1.call-start
  6.5 28.2 copy.12
  34.8 0.0 all-gather.3.cloned.1.call-update
  34.8 0.0 reduce-scatter.12.cloned.1.call-start
  34.8 713.8 %all-gather.3.cloned.1.call-done = bf16[8192,5120]{0,1:T(8,128)(2,1)} async-done(((bf16[2048,5120]{0,1:T(8,128)(2,1)}), bf16[8192,5120]{0,1:T(8,128)(2,1)}) %all-gather.3.cloned.1.call-update) | async-done | bytes 83886096 | tf_op jit(solution)/shard_map/all_gather | solution.py:14
  748.6 136.6 %all_to_all.24 = bf16[8192,2,2560]{0,2,1:T(8,128)(2,1)} all-to-all(bf16[8192,2,2560]{0,2,1:T(8,128)(2,1)} %bitcast), channel_id=1, replica_groups=mesh['tp'=4,'dp'=2] {'dp'}, dimensions={1} | all-to-all | bytes 167772160 | tf_op jit(solution)/shard_map/all_to_all | solution.py:15
  885.2 98.5 %copy.14 = bf16[2,8192,2560]{2,1,0:T(8,128)(2,1)} copy(bf16[2,8192,2560]{1,2,0:T(8,128)(2,1)} %bitcast.1) | data formatting | bytes 167772160 | tf_op jit(solution)/shard_map/all_to_all | solution.py:15
  983.7 315.6 %convolution_convert_fusion.1 = bf16[16384,3456]{1,0:T(8,128)(2,1)} fusion(bf16[16384,2560]{1,0:T(8,128)(2,1)} %bitcast.2, bf16[2560,3456]{1,0:T(8,128)(2,1)} %param.5), kind=kOutput, calls=%fused_computation.3 | convolution fusion | flops 289966915584 | bytes 214827008 | tf_op jit(solution)/shard_map/dot_general | solution.py:16
  1299.2 0.0 reduce-scatter.12.cloned.1.call-update
  1299.3 0.2 reduce-scatter.14.cloned.1.call-start
  1299.5 315.6 %convolution_convert_fusion = bf16[16384,3456]{1,0:T(8,128)(2,1)} fusion(bf16[16384,2560]{1,0:T(8,128)(2,1)} %bitcast.2, bf16[2560,3456]{1,0:T(8,128)(2,1)} %param.6), kind=kOutput, calls=%fused_computation.2 | convolution fusion | flops 289966915584 | bytes 214827008 | tf_op jit(solution)/shard_map/dot_general | solution.py:17
  1615.1 0.0 reduce-scatter.14.cloned.1.call-update
  1615.1 0.0 all-gather.5.cloned.1.call-start
  1615.2 0.0 reduce-scatter.12.cloned.1.call-done
  1615.2 100.8 %reduce-scatter.14.cloned.1.call-done = bf16[8192,3456]{1,0:T(8,128)(2,1)} async-done(((bf16[16384,3456]{1,0:T(8,128)(2,1)}), bf16[8192,3456]{1,0:T(8,128)(2,1)}) %reduce-scatter.14.cloned.1.call-update) | async-done | bytes 56623120
  1716.0 55.9 %fusion.4 = bf16[8192,3456]{1,0:T(8,128)(2,1)} fusion(bf16[8192,3456]{1,0:T(8,128)(2,1)} %reduce-scatter.14.cloned.1.call-done, bf16[8192,3456]{1,0:T(8,128)(2,1)} %reduce-scatter.12.cloned.1.call-done), kind=kLoop, calls=%fused_computation.8 | loop fusion | flops 226492416 | bytes 169869312 | tf_op jit(solution)/shard_map/convert_element_type | solution.py:20
  1771.9 0.0 all-gather.5.cloned.1.call-update
  1771.9 0.3 all-reduce.5.cloned.1.call-start
  1772.2 150.2 %all-gather.5.cloned.1.call-done = bf16[16384,3456]{1,0:T(8,128)(2,1)} async-done(((bf16[8192,3456]{1,0:T(8,128)(2,1)}), bf16[16384,3456]{1,0:T(8,128)(2,1)}) %all-gather.5.cloned.1.call-update) | async-done | bytes 113246224 | tf_op jit(solution)/shard_map/all_gather | solution.py:21
  1922.4 315.3 %convolution_convert_fusion.2 = bf16[16384,2560]{1,0:T(8,128)(2,1)} fusion(bf16[16384,3456]{1,0:T(8,128)(2,1)} %all-gather.5.cloned.1.call-done, bf16[3456,2560]{1,0:T(8,128)(2,1)} %param.7), kind=kOutput, calls=%fused_computation.9 | convolution fusion | flops 289952235520 | bytes 214827008 | tf_op jit(solution)/shard_map/dot_general | solution.py:22
  2237.6 0.0 copy-start
  2237.6 0.0 all-reduce.5.cloned.1.call-update
  2237.7 0.6 copy-done
  2238.3 0.7 dynamic-slice.4
  2239.0 1379.3 %all-reduce.5.cloned.1.call-done = bf16[2,4,2048,2560]{3,2,1,0:T(8,128)(2,1)} async-done(((bf16[2,4,2048,2560]{3,2,1,0:T(8,128)(2,1)}), bf16[2,4,2048,2560]{3,2,1,0:T(8,128)(2,1)}) %all-reduce.5.cloned.1.call-update) | async-done | bytes 83886096
  3618.2 17.9 constant_dynamic-slice_fusion
  3636.1 26.8 copy.15
  3662.9 22.8 all_to_all.25
  3685.7 20.2 fusion.5
  3705.9 25.9 copy.16
Async XLA Ops:
  6.5 742.1 %all-gather.3.cloned.1.call-start = ((), (), s32[]{:S(2)}) async-start(), calls=%async_computation.4 | async-start | bytes 104857600 | tf_op jit(solution)/shard_map/all_gather | solution.py:14
  34.8 1580.4 %reduce-scatter.12.cloned.1.call-start = ((), (), s32[]{:S(2)}) async-start(), calls=%async_computation.7 | async-start | bytes 169869312
  1299.3 416.7 %reduce-scatter.14.cloned.1.call-start = ((), (), s32[]{:S(2)}) async-start(), calls=%async_computation.8 | async-start | bytes 169869312
  1615.1 307.3 %all-gather.5.cloned.1.call-start = ((), (), s32[]{:S(2)}) async-start(), calls=%async_computation.5 | async-start | bytes 169869312 | tf_op jit(solution)/shard_map/all_gather | solution.py:21
  1771.9 1846.3 %all-reduce.5.cloned.1.call-start = ((), (), s32[]{:S(2)}) async-start(), calls=%async_computation.6 | async-start | bytes 167772160
  2237.6 0.7 copy-start
Sparse Core Ops, SparseCore 0:
  34.9 713.6 all-gather.2
  1299.4 100.6 reduce-scatter.11
  1615.2 100.6 reduce-scatter.13
  1772.0 150.3 all-gather.4
  2237.8 1380.3 all-reduce.4
where the time goes:
time: 3750 us; the launch traced here: 3740 us
  waiting for transfers between devices  2340 us (62%)
  matrix products  946 us (25%)
  local copies, waits for them, and re-layouts  199 us (5%)
  blocking collectives  159 us (4%)
  other arithmetic  76.1 us (2%)
    unnamed x8, waiting for transfers between devices  1480 us
    all_gather x1, waiting for transfers between devices, body(): xt = lax.all_gather(x, 'tp', axis=0, tiled=True)  714 us
    dot_general x1, matrix products, body(): jnp.dot(xc, wu, preferred_element_type=jnp.float32).astype(jnp.bfloat16)  316 us
    dot_general x1, matrix products, body(): jnp.dot(xc, wg, preferred_element_type=jnp.float32).astype(jnp.bfloat16)  316 us
    dot_general x1, matrix products, body(): jnp.dot(hg, wd, preferred_element_type=jnp.float32).astype(jnp.bfloat16)  315 us
    all_gather x1, waiting for transfers between devices, body(): hg = lax.all_gather(h, 'dp', axis=0, tiled=True)  150 us
    all_to_all x1, blocking collectives, body(): xc = lax.all_to_all(xt, 'dp', 1, 0, tiled=True)  137 us
    all_to_all x1, local copies, waits for them, and re-layouts, body(): xc = lax.all_to_all(xt, 'dp', 1, 0, tiled=True)  98.5 us
  transfers between devices with their start and end apart: 5, of which 4 were waited for; matrix products, arithmetic and copies ran while one was open for 8% of the time, Pallas kernels for 0%

commit v1 on v0

v1 whole, which is shorter than its diff:
```python
import jax
import jax.numpy as jnp
from jax import lax
from jax.experimental import pallas as pl
from jax.experimental.pallas import tpu as pltpu
from jax.sharding import PartitionSpec as P

MESH = pl.DeviceIdType.MESH
M = 1024
C = 256
FT = 256
WC = 512
S = 128
NC = 1280

BLOCKS = (
    ("bx0", "bx1", "ay0", "ay1"),
    ("ad0", "ad1", "bd0", "bd1"),
    ("bx2", "bx3", "ay2", "ay3"),
    ("ad2", "ad3", "bd2", "bd3"),
    ("ax0", "ax1", "by0", "by1"),
    ("ax2", "ax3", "by2", "by3"),
)
PLACE = {name: (b, q) for b, names in enumerate(BLOCKS) for q, name in enumerate(names)}

GATHER = {
    -1: (("ax0", "bx0", "ax1"), ("by0", "ay0", "by1")),
    7: (("bd0",), ("ad0",)),
    13: (("bx1",), ("ay1",)),
    20: (("ax2",), ("by2",)),
    27: (("bd1",), ("ad1",)),
    28: (("bx2",), ("ay2",)),
    34: (("ax3",), ("by3",)),
    41: (("bx3",), ("ay3",)),
    48: (("bd2",), ("ad2",)),
    55: (("bd3",), ("ad3",)),
}
REDUCE = {
    3: (("bd0", "bd1", "bx0", "bx1"), ("ad0", "ad1", "ay0", "ay1")),
    5: (("bd2", "bd3", "bx2", "bx3"), ("ad2", "ad3", "ay2", "ay3")),
    6: (("ax0", "ax1"), ("by0", "by1")),
    7: (("ax2", "ax3"), ("by2", "by3")),
}


def kernel(x, wg, wu, wd, out, gath, prod, part, near, far, pg, pu, pd,
           xv, acc, gv, uv, dv, hv, ov, rv,
           g_send, g_recv, r_send, r_recv, w_send, w_recv, w_load, x_load, o_sem, r_load, f_sem):
    tp, dp = lax.axis_index("tp"), lax.axis_index("dp")
    nx = tp + 1 - 2 * (tp % 2)
    ny = tp + 2 - 4 * (tp // 2)
    half = x.shape[0] // 2
    kd, ff = wg.shape
    dc = wd.shape[1]
    nf = pl.cdiv(ff, FT)
    to_x, to_y, to_core = {"tp": nx}, {"tp": ny}, {"dp": 1 - dp}

    barrier = pltpu.get_barrier_semaphore()
    for who in (to_x, to_y, to_core):
        pl.semaphore_signal(barrier, inc=1, device_id=who, device_id_type=MESH)
    pl.semaphore_wait(barrier, 3)

    def link_of(name):
        return to_x if name[:2] in ("ax", "bx", "bd") else to_y

    def gather(name):
        who = link_of(name)
        b, q = PLACE[name]
        n = int(name[2])
        if name[1] == "d":
            fb, fq = PLACE[("b" if name[0] == "b" else "a") + ("y" if name[0] == "b" else "x") + name[2]]
            src = gath.at[fb, pl.ds(fq * C, C)]
        else:
            src = x.at[pl.ds((half if name[0] == "b" else 0) + n * C, C)]
        return pltpu.make_async_remote_copy(
            src_ref=src, dst_ref=gath.at[b, pl.ds(q * C, C)],
            send_sem=g_send.at[b, q], recv_sem=g_recv.at[b, q], device_id=who, device_id_type=MESH)

    def send_gather(step):
        xs, ys = GATHER[step]
        for name in (v for pair in zip(xs, ys) for v in pair):
            if name[1] == "d":
                gather(("by" if name[0] == "b" else "ax") + name[2]).wait_recv()
        for name in (v for pair in zip(xs, ys) for v in pair):
            gather(name).start()

    def reduce(name):
        b, q = PLACE[name]
        n = int(name[2])
        own = (4 if name[0] == "b" else 0) + n
        if name[1] == "d":
            dst = part.at[n // 2, pl.ds(((2 if name[0] == "b" else 0) + n % 2) * C, C)]
        elif name[:2] in ("ay", "bx"):
            dst = near.at[own]
        else:
            dst = far.at[own]
        who = link_of(name)
        return pltpu.make_async_remote_copy(
            src_ref=prod.at[b + 2, pl.ds(q * C, C)], dst_ref=dst,
            send_sem=r_send.at[b, q], recv_sem=r_recv.at[b, q], device_id=who, device_id_type=MESH)

    def weights(k, j):
        width = min(WC, ff - j * WC)
        span = pl.ds(j * WC, width)
        ref, peer = ((wg, pg), (wu, pu), (wd, pd))[k]
        at = (span,) if k == 2 else (slice(None), span)
        return pltpu.make_async_remote_copy(
            src_ref=ref.at[at], dst_ref=peer.at[at], send_sem=w_send.at[k, j], recv_sem=w_recv.at[k, j],
            device_id=to_core, device_id_type=MESH)

    nw = pl.cdiv(ff, WC)
    send_gather(-1)
    for j in range(nw):
        for k in range(3):
            weights(k, j).start()

    def load_weights(f, slot):
        at = pl.multiple_of(lax.min(f * FT, ff - FT), 128)
        copies = []
        for k, (ref, peer, dst) in enumerate(((wg, pg, gv), (wu, pu, uv))):
            for m, (src, core) in enumerate(((ref, dp), (peer, 1 - dp))):
                rows = pl.ds(pl.multiple_of(core * kd, 128), kd)
                copies.append(pltpu.make_async_copy(
                    src.at[:, pl.ds(at, FT)], dst.at[slot, rows], w_load.at[slot, 2 * k + m]))
        for m, (src, core) in enumerate(((wd, dp), (pd, 1 - dp))):
            cols = pl.ds(pl.multiple_of(core * dc, 128), dc)
            copies.append(pltpu.make_async_copy(
                src.at[pl.ds(at, FT)], dv.at[slot, :, cols], w_load.at[slot, 4 + m]))
        return copies

    def await_weights(j):
        for k in range(3):
            weights(k, j).wait_recv()

    def load_own(i, q):
        at = pl.multiple_of(lax.min(i, 1) * M + q * C, C)
        return pltpu.make_async_copy(x.at[pl.ds(at, C)], xv.at[pl.ds(q * C, C)], x_load.at[q])

    def load_rows(b, q):
        rows = pl.ds(q * C, C)
        return pltpu.make_async_copy(gath.at[b, rows], xv.at[rows], x_load.at[q])

    def start_rows(i):
        @pl.when(i < 2)
        def _():
            for q in range(M // C):
                load_own(i, q).start()
        for b in range(len(BLOCKS)):
            @pl.when(i == b + 2)
            def _():
                for q, name in enumerate(BLOCKS[b]):
                    if name[:2] not in ("ax", "by"):
                        gather(name).wait_recv()
                    load_rows(b, q).start()

    start_rows(jnp.int32(0))
    await_weights(0)
    for copy in load_weights(jnp.int32(0), 0):
        copy.start()

    def store(i, r, slot):
        return pltpu.make_async_copy(ov.at[slot], prod.at[i, pl.ds(pl.multiple_of(r * S, S), S)], o_sem.at[slot])

    def load_part(i, r, slot):
        return pltpu.make_async_copy(part.at[lax.max(i - 6, 0), pl.ds(pl.multiple_of(r * S, S), S)], rv.at[slot], r_load.at[slot])

    @pl.loop(0, len(BLOCKS) + 2)
    def _(i):
        acc[...] = jnp.zeros_like(acc)
        for q in range(M // C):
            load_own(i, q).wait()

        @pl.loop(0, nf)
        def _(f):
            step = i * nf + f
            slot = step % 2
            for at in GATHER:
                if at >= 0:
                    @pl.when(step == at)
                    def _():
                        send_gather(at)
            for j in range(1, nw):
                @pl.when(step == j * WC // FT - 1)
                def _():
                    await_weights(j)
            for copy in load_weights(f, slot):
                copy.wait()

            @pl.when(step + 1 < (len(BLOCKS) + 2) * nf)
            def _():
                for copy in load_weights((f + 1) % nf, 1 - slot):
                    copy.start()
            a = jnp.dot(xv[...], gv[slot], preferred_element_type=jnp.float32)
            b = jnp.dot(xv[...], uv[slot], preferred_element_type=jnp.float32)
            skip = lax.max(f * FT - (ff - FT), 0)
            fresh = lax.broadcasted_iota(jnp.int32, (M, FT), 1) >= skip
            h = a * jax.nn.sigmoid(a) * b
            hv[...] = jnp.where(fresh, h, 0.0).astype(jnp.bfloat16)
            for n in range(0, acc.shape[1], NC):
                cols = slice(n, n + NC)
                acc[:, cols] += jnp.dot(hv[...], dv[slot, :, cols], preferred_element_type=jnp.float32)

        late = i >= 6
        for k in range(2):
            @pl.when(i == 6 + k)
            def _():
                for q in range(2):
                    reduce("ad" + str(2 * k + q)).wait_recv()
                    reduce("bd" + str(2 * k + q)).wait_recv()
        @pl.when(late)
        def _():
            load_part(i, 0, 0).start()

        @pl.loop(0, M // S)
        def _(r):
            slot = r % 2
            rows = pl.ds(pl.multiple_of(r * S, S), S)

            @pl.when(r >= 2)
            def _():
                store(i, r - 2, slot).wait()

            @pl.when(late)
            def _():
                @pl.when(r + 1 < M // S)
                def _():
                    load_part(i, r + 1, 1 - slot).start()
                load_part(i, r, slot).wait()
                ov[slot] = (acc[rows] + rv[slot].astype(jnp.float32)).astype(jnp.bfloat16)

            @pl.when(jnp.logical_not(late))
            def _():
                ov[slot] = acc[rows].astype(jnp.bfloat16)
            store(i, r, slot).start()
        for slot in range(2):
            store(i, M // S - 2 + slot, slot).wait()

        for at in REDUCE:
            @pl.when(i == at)
            def _():
                for pair in zip(*REDUCE[at]):
                    for name in pair:
                        reduce(name).start()

        @pl.when(i + 1 < len(BLOCKS) + 2)
        def _():
            start_rows(i + 1)

    order = [half_ + str(n) for n in range(4) for half_ in "ab"]

    def parts(name):
        own = (4 if name[0] == "b" else 0) + int(name[1])
        srcs = (prod.at[own // 4, pl.ds((own % 4) * C, C)], near.at[own], far.at[own])
        return [pltpu.make_async_copy(src, xv.at[pl.ds(m * C, C)], f_sem.at[m]) for m, src in enumerate(srcs)]

    def result(name):
        n = int(name[1])
        return pltpu.make_async_copy(
            xv.at[pl.ds(3 * C, C)], out.at[pl.ds((half if name[0] == "b" else 0) + n * C, C)], f_sem.at[3])

    for t, name in enumerate(order):
        n = name[1]
        reduce(("ay" if name[0] == "a" else "bx") + n).wait_recv()
        reduce(("ax" if name[0] == "a" else "by") + n).wait_recv()
        copies = parts(name)
        for copy in copies:
            copy.start()
        for copy in copies:
            copy.wait()
        if t:
            result(order[t - 1]).wait()

        @pl.loop(0, C // 32)
        def _(r):
            rows = [pl.ds(pl.multiple_of(m * C + r * 32, 32), 32) for m in range(4)]
            f32 = jnp.float32
            xv[rows[3]] = (xv[rows[0]].astype(f32) + xv[rows[1]].astype(f32) + xv[rows[2]].astype(f32)).astype(jnp.bfloat16)
        result(name).start()
    result(order[-1]).wait()

    for name in PLACE:
        gather(name).wait_send()
        reduce(name).wait_send()
    for j in range(nw):
        for k in range(3):
            weights(k, j).wait_send()


def solution(mesh):
    def body(x, wg, wu, wd):
        r, d = x.shape
        kd, ff = wg.shape
        dc = wd.shape[1]
        bf = jnp.bfloat16
        any_ = pl.BlockSpec(memory_space=pl.ANY)
        nb = len(BLOCKS)
        nw = -(-ff // WC)
        shapes = [(r, d), (nb, M, d), (nb + 2, M, d), (2, M, d), (r // C, C, d), (r // C, C, d), (kd, ff), (kd, ff), (ff, dc)]
        dma = pltpu.SemaphoreType.DMA
        outs = pl.pallas_call(
            kernel,
            out_shape=[jax.ShapeDtypeStruct(s, bf) for s in shapes],
            in_specs=[any_] * 4,
            out_specs=[any_] * len(shapes),
            scratch_shapes=[
                pltpu.VMEM((M, d), bf), pltpu.VMEM((M, d), jnp.float32),
                pltpu.VMEM((2, d, FT), bf), pltpu.VMEM((2, d, FT), bf), pltpu.VMEM((2, FT, d), bf),
                pltpu.VMEM((M, FT), bf), pltpu.VMEM((2, S, d), bf), pltpu.VMEM((2, S, d), bf),
                dma((nb, M // C)), dma((nb, M // C)), dma((nb, M // C)), dma((nb, M // C)),
                dma((3, nw)), dma((3, nw)), dma((2, 6)), dma((M // C,)), dma((2,)), dma((2,)), dma((4,)),
            ],
            compiler_params=pltpu.CompilerParams(collective_id=0, has_side_effects=True, vmem_limit_bytes=67043328),
        )(x, wg, wu, wd)
        return (x.astype(jnp.float32) + outs[0].astype(jnp.float32)).astype(bf)

    return jax.shard_map(body, mesh=mesh, in_specs=(P(("dp", "tp"), None), P("dp", "tp"), P("dp", "tp"), P("tp", "dp")), out_specs=P(("dp", "tp"), None), check_vma=False)
```

time: 3750 us -> 1390 us (0.37)
  waiting for transfers between devices: 2340 us -> 0 us
  Pallas kernels: 0 us -> 1370 us
  matrix products: 946 us -> 0 us
  local copies, waits for them, and re-layouts: 199 us -> 0 us
  blocking collectives: 159 us -> 0 us
  other arithmetic: 76.1 us -> 25 us
    unnamed x8 -> x0, waiting for transfers between devices: 1480 us -> none
    pallas_call x0 -> x1, Pallas kernels: none -> 1370 us  [body(): pl.pallas_call(kernel, out_shape=[jax.ShapeDtypeStruct(s, bf) for s in sh...]
    dot_general x3 -> x0, matrix products: 946 us -> none  [the longest x1 316 us: body(): jnp.dot(xc, wu, preferred_element_type=jnp.float32).astype(jnp.bfloat16)]
    all_gather x2 -> x0, waiting for transfers between devices: 864 us -> none  [the longest x1 714 us: body(): xt = lax.all_gather(x, 'tp', axis=0, tiled=True)]
    all_to_all x2 -> x0, blocking collectives: 159 us -> none  [the longest x1 137 us: body(): xc = lax.all_to_all(xt, 'dp', 1, 0, tiled=True)]
    all_to_all x1 -> x0, local copies, waits for them, and re-layouts: 98.5 us -> none  [body(): xc = lax.all_to_all(xt, 'dp', 1, 0, tiled=True)]
    convert_element_type x2 -> x1, other arithmetic: 76.1 us -> 25 us  [body(): return (x.astype(jnp.float32) + outs[0].astype(jnp.float32)).astype(bf)]
    unnamed x5 -> x0, local copies, waits for them, and re-layouts: 47.4 us -> none
  transfers between devices with their start and end apart: 5 -> 0, of which waited for: 4 -> 0; matrix products, arithmetic and copies ran while one was open for 8% -> 0% of each run, Pallas kernels for 0% -> 0%
where the time goes in v1:
time: 1390 us
  Pallas kernels  1370 us (99%)
  other arithmetic  25 us (2%)
    pallas_call x1, Pallas kernels, body(): pl.pallas_call(kernel, out_shape=[jax.ShapeDtypeStruct(s, bf) for s in sh...  1370 us

profile of v1, /device:TPU:0, one launch (start us, length us, event | category | flops | bytes accessed | tf_op | source)
XLA Modules:
  0.0 1391.7 jit_solution(5187947047781691031)
XLA Ops:
  0.0 1366.6 %shard_map.46 = (bf16[2048,5120]{1,0:T(8,128)(2,1)}, bf16[6,1024,5120]{2,1,0:T(8,128)(2,1)}, bf16[8,1024,5120]{2,1,0:T(8,128)(2,1)}, bf16[2,1024,5120]{2,1,0:T(8...) custom-call(bf16[2048,5120]{1,0:T(8,128)(2,1)} %x.1, ...), custom_call_target="tpu_custom_call" | custom-call | tf_op jit(solution)/shard_map/pallas_call | solution.py:300
  1366.6 25.0 %add_convert_fusion = bf16[2048,5120]{1,0:T(8,128)(2,1)} fusion(bf16[2048,5120]{1,0:T(8,128)(2,1)} %get-tuple-element.6, bf16[2048,5120]{1,0:T(8,128)(2,1)} %x.1), kind=kLoop, calls=%fused_computation | loop fusion | flops 41943040 | bytes 62914560 | tf_op jit(solution)/shard_map/convert_element_type | solution.py:314

commit v2 on v1

--- a/solution.py
+++ b/solution.py
@@ -12,6 +12,7 @@
 WC = 512
 S = 128
 NC = 1280
+R = 32
 
 BLOCKS = (
     ("bx0", "bx1", "ay0", "ay1"),
@@ -43,8 +44,8 @@
 }
 
 
-def kernel(x, wg, wu, wd, out, gath, prod, part, near, far, pg, pu, pd,
-           xv, acc, gv, uv, dv, hv, ov, rv,
+def kernel(x, wg, wu, wd, xv, acc, gath, prod, part, near, far, pg, pu, pd,
+           gv, uv, dv, hv, ov, rv,
            g_send, g_recv, r_send, r_recv, w_send, w_recv, w_load, x_load, o_sem, r_load, f_sem):
     tp, dp = lax.axis_index("tp"), lax.axis_index("dp")
     nx = tp + 1 - 2 * (tp % 2)
@@ -246,37 +247,77 @@
         def _():
             start_rows(i + 1)
 
-    order = [half_ + str(n) for n in range(4) for half_ in "ab"]
-
-    def parts(name):
-        own = (4 if name[0] == "b" else 0) + int(name[1])
-        srcs = (prod.at[own // 4, pl.ds((own % 4) * C, C)], near.at[own], far.at[own])
-        return [pltpu.make_async_copy(src, xv.at[pl.ds(m * C, C)], f_sem.at[m]) for m, src in enumerate(srcs)]
-
-    def result(name):
-        n = int(name[1])
-        return pltpu.make_async_copy(
-            xv.at[pl.ds(3 * C, C)], out.at[pl.ds((half if name[0] == "b" else 0) + n * C, C)], f_sem.at[3])
-
-    for t, name in enumerate(order):
-        n = name[1]
-        reduce(("ay" if name[0] == "a" else "bx") + n).wait_recv()
-        reduce(("ax" if name[0] == "a" else "by") + n).wait_recv()
-        copies = parts(name)
+    f32 = jnp.float32
+
+    def own_of(name):
+        return (4 if name[0] == "b" else 0) + int(name[1])
+
+    def pieces(name):
+        own = own_of(name)
+        src = pl.ds((half if name[0] == "b" else 0) + int(name[1]) * C, C)
+        copies = [pltpu.make_async_copy(prod.at[own // 4, pl.ds((own % 4) * C, C)], dv.at[0], f_sem.at[0]),
+                  pltpu.make_async_copy(near.at[own], dv.at[1], f_sem.at[1])]
+        for m in range(2):
+            part_ = pl.ds(src.start + m * S, S)
+            copies.append(pltpu.make_async_copy(x.at[part_], ov.at[m], f_sem.at[2 + m]))
+        return copies
+
+    def late_piece(name, m, to):
+        sem = f_sem.at[(4 if to is rv else 2) + m]
+        return pltpu.make_async_copy(far.at[own_of(name), pl.ds(m * S, S)], to.at[m], sem)
+
+    def await_near(name):
+        reduce(("ay" if name[0] == "a" else "bx") + name[1]).wait_recv()
+
+    def await_far(name):
+        reduce(("ax" if name[0] == "a" else "by") + name[1]).wait_recv()
+
+    def place(name):
+        return (2 * C if name[0] == "b" else 0) + int(name[1]) % 2 * C
+
+    def run(copies):
         for copy in copies:
             copy.start()
         for copy in copies:
             copy.wait()
-        if t:
-            result(order[t - 1]).wait()
-
-        @pl.loop(0, C // 32)
-        def _(r):
-            rows = [pl.ds(pl.multiple_of(m * C + r * 32, 32), 32) for m in range(4)]
-            f32 = jnp.float32
-            xv[rows[3]] = (xv[rows[0]].astype(f32) + xv[rows[1]].astype(f32) + xv[rows[2]].astype(f32)).astype(jnp.bfloat16)
-        result(name).start()
-    result(order[-1]).wait()
+
+    def rows_of(base, r):
+        return pl.ds(pl.multiple_of(base + r * R, R), R)
+
+    for name in ("a2", "b2", "a3", "b3"):
+        await_near(name)
+        run(pieces(name))
+        for m in range(2):
+            @pl.loop(0, S // R)
+            def _(r):
+                at, here = rows_of(m * S, r), rows_of(0, r)
+                acc[rows_of(place(name) + m * S, r)] = (
+                    dv[0, at].astype(f32) + dv[1, at].astype(f32) + ov[m, here].astype(f32))
+    for name in ("a0", "b0", "a1", "b1"):
+        await_near(name)
+        await_far(name)
+        run(pieces(name) + [late_piece(name, m, rv) for m in range(2)])
+        for m in range(2):
+            @pl.loop(0, S // R)
+            def _(r):
+                at, here = rows_of(m * S, r), rows_of(0, r)
+                xv[rows_of(place(name) + m * S, r)] = (
+                    dv[0, at].astype(f32) + dv[1, at].astype(f32) + rv[m, here].astype(f32) + ov[m, here].astype(f32)
+                ).astype(jnp.bfloat16)
+    for n in ("2", "3"):
+        lates = []
+        for name, to in (("a" + n, rv), ("b" + n, ov)):
+            await_far(name)
+            for m in range(2):
+                lates.append((late_piece(name, m, to), to, place(name) + m * S, m))
+                lates[-1][0].start()
+        for copy, to, base, m in lates:
+            copy.wait()
+
+            @pl.loop(0, S // R)
+            def _(r):
+                at = rows_of(base, r)
+                acc[at] = acc[at] + to[m, rows_of(0, r)].astype(f32)
 
     for name in PLACE:
         gather(name).wait_send()
@@ -286,31 +327,58 @@
             weights(k, j).wait_send()
 
 
+def write(xv, acc, out, yv, sem):
+    half, quarter = xv.shape[0], xv.shape[0] // 2
+    early = [pltpu.make_async_copy(xv.at[pl.ds(k * quarter, quarter)], out.at[pl.ds(k * half, quarter)], sem.at[k]) for k in range(2)]
+    late = []
+    for k in range(8):
+        rows = k * S
+        to = (k // 4) * half + quarter + (k % 4) * S
+        late.append(pltpu.make_async_copy(yv.at[pl.ds(rows, S)], out.at[pl.ds(to, S)], sem.at[2 + k]))
+    for copy in early:
+        copy.start()
+    for k, copy in enumerate(late):
+        @pl.loop(0, S // R)
+        def _(r):
+            at = pl.ds(pl.multiple_of(k * S + r * R, R), R)
+            yv[at] = acc[at].astype(jnp.bfloat16)
+        copy.start()
+    for copy in early + late:
+        copy.wait()
+
+
 def solution(mesh):
     def body(x, wg, wu, wd):
         r, d = x.shape
         kd, ff = wg.shape
-        dc = wd.shape[1]
-        bf = jnp.bfloat16
+        bf, f32 = jnp.bfloat16, jnp.float32
         any_ = pl.BlockSpec(memory_space=pl.ANY)
+        vmem = pl.BlockSpec(memory_space=pltpu.VMEM)
         nb = len(BLOCKS)
         nw = -(-ff // WC)
-        shapes = [(r, d), (nb, M, d), (nb + 2, M, d), (2, M, d), (r // C, C, d), (r // C, C, d), (kd, ff), (kd, ff), (ff, dc)]
+        shapes = [(nb, M, d), (nb + 2, M, d), (2, M, d), (r // C, C, d), (r // C, C, d), (kd, ff), (kd, ff), wd.shape]
         dma = pltpu.SemaphoreType.DMA
-        outs = pl.pallas_call(
+        params = dict(has_side_effects=True, vmem_limit_bytes=32 * 2**20)
+        xv, acc, *_ = pl.pallas_call(
             kernel,
-            out_shape=[jax.ShapeDtypeStruct(s, bf) for s in shapes],
+            out_shape=[pltpu.VMEM((M, d), bf), pltpu.VMEM((M, d), f32)] + [jax.ShapeDtypeStruct(s, bf) for s in shapes],
             in_specs=[any_] * 4,
-            out_specs=[any_] * len(shapes),
+            out_specs=[vmem] * 2 + [any_] * len(shapes),
             scratch_shapes=[
-                pltpu.VMEM((M, d), bf), pltpu.VMEM((M, d), jnp.float32),
                 pltpu.VMEM((2, d, FT), bf), pltpu.VMEM((2, d, FT), bf), pltpu.VMEM((2, FT, d), bf),
                 pltpu.VMEM((M, FT), bf), pltpu.VMEM((2, S, d), bf), pltpu.VMEM((2, S, d), bf),
                 dma((nb, M // C)), dma((nb, M // C)), dma((nb, M // C)), dma((nb, M // C)),
-                dma((3, nw)), dma((3, nw)), dma((2, 6)), dma((M // C,)), dma((2,)), dma((2,)), dma((4,)),
+                dma((3, nw)), dma((3, nw)), dma((2, 6)), dma((M // C,)), dma((2,)), dma((2,)), dma((6,)),
             ],
-            compiler_params=pltpu.CompilerParams(collective_id=0, has_side_effects=True, vmem_limit_bytes=67043328),
+            compiler_params=pltpu.CompilerParams(collective_id=0, **params),
         )(x, wg, wu, wd)
-        return (x.astype(jnp.float32) + outs[0].astype(jnp.float32)).astype(bf)
+        return pl.pallas_call(
+            write,
+            out_shape=jax.ShapeDtypeStruct((r, d), bf),
+            in_specs=[vmem] * 2,
+            out_specs=any_,
+            scratch_shapes=[pltpu.VMEM((M, d), bf), dma((10,))],
+            compiler_params=pltpu.CompilerParams(vmem_limit_bytes=16 * 2**20),
+        )(xv, acc)
 
     return jax.shard_map(body, mesh=mesh, in_specs=(P(("dp", "tp"), None), P("dp", "tp"), P("dp", "tp"), P("tp", "dp")), out_specs=P(("dp", "tp"), None), check_vma=False)

time: 1390 us -> 1370 us (0.986)
  other arithmetic: 25 us -> 0 us
    convert_element_type x1 -> x0, other arithmetic: 25 us -> none  [body(): return (x.astype(jnp.float32) + outs[0].astype(jnp.float32)).astype(bf)]
    pallas_call x1 -> x2, Pallas kernels: 1370 us -> 1370 us  [the longest x1 1360 us: body(): pl.pallas_call(kernel, out_shape=[pltpu.VMEM((M, d), bf), pltpu.VMEM((M,...]
where the time goes in v2:
time: 1370 us
  Pallas kernels  1370 us (100%)
    pallas_call x1, Pallas kernels, body(): pl.pallas_call(kernel, out_shape=[pltpu.VMEM((M, d), bf), pltpu.VMEM((M,...  1360 us

profile of v2, /device:TPU:0, one launch (start us, length us, event | category | flops | bytes accessed | tf_op | source)
XLA Modules:
  0.0 1365.0 jit_solution(3938190759744569754)
XLA Ops:
  0.0 1357.8 %shard_map.46 = (bf16[1024,5120]{1,0:T(8,128)(2,1)S(1)}, f32[1024,5120]{1,0:T(8,128)S(1)}, bf16[6,1024,5120]{2,1,0:T(8,128)(2,1)}, bf16[8,1024,5120]{2,1,0:T(8,1...) custom-call(bf16[2048,5120]{1,0:T(8,128)(2,1)} %x.1, ...), custom_call_target="tpu_custom_call" | custom-call | tf_op jit(solution)/shard_map/pallas_call | solution.py:362
  1357.8 7.2 shard_map.47

commit v3 on v0

v3 whole, which is shorter than its diff:
```python
import jax
import jax.numpy as jnp
from jax import lax
from jax.experimental import pallas as pl
from jax.experimental.pallas import tpu as pltpu
from jax.sharding import PartitionSpec as P

MESH = pl.DeviceIdType.MESH
M = 1024
FT = 256
NF = 14
C = 256
WC = 384
NC = 1280
MS = 512
R = 32
L0 = 6
V0 = 11

O1, O2, N1, N2 = range(4)
MINE, YS, LATE = range(3)
JOBS = (
    (O1, MINE, 0, 14, 1, 1, "zs"),
    (O2, MINE, 0, 14, 1, 1, "zs"),
    (N1, MINE, 0, 14, 1, 1, "z-"),
    (N1, YS, 0, 5, 1, 1, "k-"),
    (O1, YS, 0, 5, 1, 0, "k-"),
    (O2, YS, 0, 5, 1, 0, "k-"),
    (N1, YS, 5, 1, 1, 1, "kr"),
    (N2, MINE, 0, 14, 1, 1, "z-"),
    (N2, YS, 0, 7, 1, 1, "k-"),
    (N1, YS, 6, 2, 1, 0, "k-"),
    (O1, YS, 5, 3, 1, 0, "k-"),
    (O2, YS, 5, 3, 1, 0, "k-"),
    (N2, YS, 7, 2, 1, 1, "kr"),
    (O1, YS, 0, 8, 0, 1, "ls"),
    (O2, YS, 0, 8, 0, 1, "ls"),
    (N1, YS, 8, 2, 1, 0, "k-"),
    (N2, YS, 9, 1, 1, 0, "k-"),
    (O1, YS, 8, 2, 1, 0, "k-"),
    (O2, YS, 8, 2, 1, 0, "k-"),
    (N1, YS, 10, 1, 1, 0, "k-"),
    (O1, YS, 10, 1, 1, 0, "k-"),
    (O2, YS, 10, 1, 1, 0, "k-"),
    (O1, YS, 8, 3, 0, 1, "l-"),
    (O1, LATE, 6, 2, 0, 1, "ks"),
    (N1, YS, 11, 1, 1, 0, "k-"),
    (O1, YS, 11, 1, 1, 0, "k-"),
    (O2, YS, 11, 1, 1, 0, "k-"),
    (O2, YS, 8, 4, 0, 1, "ls"),
    (N1, YS, 12, 1, 1, 0, "k-"),
    (O1, YS, 12, 1, 1, 0, "k-"),
    (O2, YS, 12, 1, 1, 0, "k-"),
    (N1, YS, 13, 1, 1, 0, "k-"),
    (N2, YS, 10, 4, 1, 0, "k-"),
    (O1, YS, 13, 1, 1, 0, "k-"),
    (O2, YS, 13, 1, 1, 0, "k-"),
    (O1, YS, 11, 3, 0, 1, "l-"),
    (O1, LATE, 8, 6, 0, 1, "k-"),
    (O2, YS, 12, 2, 0, 1, "l-"),
    (O2, LATE, 9, 5, 0, 1, "k-"),
)
NJ = len(JOBS)
AHEAD = {2: (0, 1), 3: (2, 3), 8: (6,)}
FORWARD = {9: (6, 7), 15: (8, 9), 19: (10,)}
TURN = 8
SPREAD = {17: (6, 7), 32: (8, 9), 36: (10, 11, 12, 13)}
FINAL = (22, 27)
LEAVE = 36


def plan():
    slots, new, ahead, fresh = [], [], [], []
    group, last, seen, firsts = -1, None, 0, []
    for j, (rows, src, f0, n, s1, s2, _) in enumerate(JOBS):
        starts = bool(s1 and rows != last)
        if starts:
            group, last = group + 1, rows
            firsts.append(j)
        slots.append(max(group, 0) % 2)
        new.append(int(starts))
        top = f0 + n
        fresh.append(max(seen, f0) if src == YS and s1 and top > seen else NF)
        if src == YS and s1:
            seen = max(seen, top)
    late = 2
    load = [-1] * NJ
    for a, b in zip(firsts, firsts[1:]):
        load[b if b == late else a] = JOBS[b][0]
    return slots, new, load, fresh


SLOT, NEW, LOAD, FRESH = plan()


def kernel(x, wg, wu, wd, xv, acc, gn, pg, pu, pd, yg, yu, yd, ld, xd, ho, hs, hr, sv, prod, part,
           gv, uv, dv, hv,
           y_send, y_recv, d_send, d_recv, w_send, w_recv, l_send, l_recv, e_send, e_recv, n_send, n_recv,
           r_send, r_recv, h_send, h_recv, t_sem, w_load, x_load, s_sem, h_sem, o_sem):
    tp, dp = lax.axis_index("tp"), lax.axis_index("dp")
    to_x = {"tp": tp + 1 - 2 * (tp % 2)}
    to_y = {"tp": tp + 2 - 4 * (tp // 2)}
    to_core = {"dp": 1 - dp}
    kd, ff = wg.shape
    dc = wd.shape[1]
    f32, bf16 = jnp.float32, jnp.bfloat16
    last = (NF - 1) * FT
    own_rows = x.shape[0]

    barrier = pltpu.get_barrier_semaphore()
    for who in (to_x, to_y, to_core):
        pl.semaphore_signal(barrier, inc=1, device_id=who, device_id_type=MESH)
    pl.semaphore_wait(barrier, 3)

    def remote(src, dst, send, recv, who):
        return pltpu.make_async_remote_copy(
            src_ref=src, dst_ref=dst, send_sem=send, recv_sem=recv, device_id=who, device_id_type=MESH)

    def pick(values, j):
        got = jnp.int32(values[0])
        for k, v in enumerate(values):
            if v != values[0]:
                got = jnp.where(j == k, v, got)
        return got

    def col(t):
        return t * FT if isinstance(t, int) else pl.multiple_of(t * FT, FT)

    def tokens(q):
        return remote(x.at[pl.ds(q * C, C)], gn.at[q // (M // C), pl.ds(q % (M // C) * C, C)], n_send.at[q], n_recv.at[q], to_x)

    def mine(k, c):
        at = c * WC if isinstance(c, int) else pl.multiple_of(c * WC, WC)
        ref, peer = ((wg, pg), (wu, pu), (wd, pd))[k]
        ix = (pl.ds(at, WC),) if k == 2 else (slice(None), pl.ds(at, WC))
        return remote(ref.at[ix], peer.at[ix], w_send.at[k, c], w_recv.at[k, c], to_core)

    def y_tile(k, t, width):
        ref, mirror = ((wg, yg), (wu, yu), (wd, yd))[k]
        span = pl.ds(col(t), width)
        return ref.at[(span,) if k == 2 else (slice(None), span)], mirror.at[(0, span) if k == 2 else (0, slice(None), span)], mirror.at[(1, span) if k == 2 else (1, slice(None), span)]

    def along_y(k, t, width=FT):
        src, dst, _ = y_tile(k, t, width)
        return remote(src, dst, y_send.at[k, t], y_recv.at[k, t], to_y)

    def across(k, t, width=FT):
        _, src, dst = y_tile(k, t, width)
        return remote(src, dst, d_send.at[k, t], d_recv.at[k, t], to_core)

    def width_of(t):
        return ff - last if t == NF - 1 else FT

    def late_rows(t):
        return pl.ds(col(t - L0), width_of(t) if isinstance(t, int) else FT)

    def late_send(t):
        if t < V0:
            return remote(yd.at[0, pl.ds(col(t), FT)], ld.at[0, late_rows(t)], l_send.at[t - L0], l_recv.at[t - L0], to_x)
        return remote(xd.at[pl.ds(col(t - V0), width_of(t))], ld.at[0, late_rows(t)], l_send.at[t - L0], l_recv.at[t - L0], to_y)

    def late_across(t, rows):
        return remote(ld.at[0, rows], ld.at[1, rows], e_send.at[t - L0], e_recv.at[t - L0], to_core)

    def turn():
        return remote(wd.at[pl.ds(V0 * FT, ff - V0 * FT)], xd, t_sem.at[0], t_sem.at[1], to_x)

    def hidden(k, t, end=False):
        at = (k, t, slice(None), pl.ds(NF * FT - ff, ff - last)) if end else (k, t)
        return remote(hs.at[at], hr.at[at], h_send.at[k, t], h_recv.at[k, t], to_x)

    def products(k, q):
        rows = pl.ds(q * C, C)
        return remote(prod.at[k, rows], part.at[k, rows], r_send.at[k, q], r_recv.at[k, q], to_x)

    for q in range(own_rows // C):
        tokens(q).start()
    turn().start()
    for t in range(NF):
        for k in range(3):
            along_y(k, t, width_of(t)).start()
    for c in range(ff // WC):
        for k in range(3):
            mine(k, c).start()

    def tile_at(f):
        return pl.multiple_of(lax.min(f * FT, ff - FT), 128)

    def halves(extent):
        return [pl.ds(pl.multiple_of(core * extent, 128), extent) for core in (dp, 1 - dp)]

    def load_first(slot, f, src):
        at = tile_at(f)
        copies = []
        for k, (pair, dst) in enumerate((((wg, pg) if src == MINE else (yg.at[0], yg.at[1]), gv),
                                         ((wu, pu) if src == MINE else (yu.at[0], yu.at[1]), uv))):
            for m, (ref, rows) in enumerate(zip(pair, halves(kd))):
                copies.append(pltpu.make_async_copy(ref.at[:, pl.ds(at, FT)], dst.at[slot, rows], w_load.at[slot, 2 * k + m]))
        return copies

    def load_second(slot, f, src):
        at = tile_at(f) if src != LATE else pl.multiple_of(tile_at(f) - L0 * FT, 128)
        pair = {MINE: (wd, pd), YS: (yd.at[0], yd.at[1]), LATE: (ld.at[0], ld.at[1])}[src]
        return [pltpu.make_async_copy(ref.at[pl.ds(at, FT)], dv.at[slot, :, cols], w_load.at[slot, 4 + m])
                for m, (ref, cols) in enumerate(zip(pair, halves(dc)))]

    def load_h(slot, rows, f, src, end=False):
        cols = pl.ds(NF * FT - ff, ff - last) if end else slice(None)
        return pltpu.make_async_copy((hr if src == LATE else ho).at[rows, f, :, cols], hv.at[slot, :, cols], w_load.at[slot, 6])

    def load_x(rows, slot):
        own = pltpu.make_async_copy(x.at[pl.ds(pl.multiple_of(lax.min(rows, 1) * M, M), M)], xv.at[slot], x_load.at[slot])
        other = pltpu.make_async_copy(gn.at[lax.max(rows - 2, 0)], xv.at[slot], x_load.at[slot])
        return own, other

    def start_x(rows, slot):
        @pl.when(rows < N1)
        def _():
            load_x(rows, slot)[0].start()

        @pl.when(rows >= N1)
        def _():
            load_x(rows, slot)[1].start()

    def send_across(t, wait_first=True):
        for k in range(3):
            along_y(k, t, width_of(t)).wait_recv()
        for k in range(3):
            across(k, t, width_of(t)).start()

    def prefetch(slot, rows, src, f, first, second, fresh):
        @pl.when((src == MINE) & (rows == O1) & (f % 3 != 2) & (f < NF - 1))
        def _():
            for k in range(3):
                mine(k, (2 * f + 2) // 3).wait_recv()

        is_new = (src == YS) & (first == 1) & (f >= fresh)
        early = [t for ts in AHEAD.values() for t in ts]
        to_send = is_new
        for t in early:
            to_send = to_send & (f != t)

        @pl.when(to_send & (f < NF - 1))
        def _():
            for k in range(3):
                along_y(k, f).wait_recv()
            for k in range(3):
                across(k, f).start()

        @pl.when(is_new & (f < NF - 1))
        def _():
            for k in range(3):
                across(k, f).wait_recv()

        @pl.when(is_new & (f == NF - 1))
        def _():
            send_across(NF - 1)
            for k in range(3):
                across(k, NF - 1, width_of(NF - 1)).wait_recv()

        @pl.when((src == LATE) & (f < NF - 1))
        def _():
            hidden(rows, f).wait_recv()

        @pl.when((src == LATE) & (f == NF - 1))
        def _():
            hidden(rows, NF - 1, True).wait_recv()
            hv[slot, :, pl.ds(0, NF * FT - ff)] = jnp.zeros((M, NF * FT - ff), bf16)
            load_h(slot, rows, NF - 1, LATE, True).start()

        @pl.when((src == LATE) & (rows == O1) & (f < NF - 1))
        def _():
            late_across(f, late_rows(f)).wait_recv()

        @pl.when((src == LATE) & (rows == O1) & (f == NF - 1))
        def _():
            late_across(NF - 1, late_rows(NF - 1)).wait_recv()

        for value in (MINE, YS):
            @pl.when((first == 1) & (src == value))
            def _():
                for copy in load_first(slot, f, value):
                    copy.start()
        for value in (MINE, YS, LATE):
            @pl.when((second == 1) & (src == value))
            def _():
                for copy in load_second(slot, f, value):
                    copy.start()
        for value in (YS, LATE):
            @pl.when((first == 0) & (src == value) & ((src == YS) | (f < NF - 1)))
            def _():
                load_h(slot, rows, f, value).start()

    def store_h(slot, rows, f):
        return (pltpu.make_async_copy(hv.at[slot], ho.at[lax.min(rows, 1), f], h_sem.at[slot]),
                pltpu.make_async_copy(hv.at[slot], hs.at[lax.max(rows - 2, 0), f], h_sem.at[slot]))

    def swap(k, out):
        return pltpu.make_async_copy(acc, sv.at[k], s_sem) if out else pltpu.make_async_copy(sv.at[k], acc, s_sem)

    def store(k, q, slot):
        rows = pl.ds(q * C, C)
        return pltpu.make_async_copy(xv.at[slot, rows], prod.at[k, rows], o_sem.at[q])

    start_x(jnp.int32(O1), 0)
    prefetch(0, jnp.int32(O1), jnp.int32(MINE), jnp.int32(0), jnp.int32(1), jnp.int32(1), jnp.int32(NF))

    columns = [[job[i] for job in JOBS] for i in range(6)]
    modes = [job[6] for job in JOBS]

    def job(j, step0):
        rows, src, f0, n, first, second = [pick(c, j) for c in columns]
        after = lax.min(j + 1, NJ - 1)
        rows_n, src_n, f0_n, _, first_n, second_n = [pick(c, after) for c in columns]
        fresh, fresh_n = pick(FRESH, j), pick(FRESH, after)
        slot_x = pick(SLOT, j)
        load_n = pick(LOAD, j)
        is_h = (first == 1) & (second == 0)
        before = lax.max(j - 1, 0)
        own_h_before = pick([int(a[4] and not a[5] and a[0] < N1) for a in JOBS], before)

        for at, tiles in AHEAD.items():
            @pl.when(j == at)
            def _():
                for t in tiles:
                    send_across(t)
        @pl.when(j == 2)
        def _():
            for q in range(M // C):
                tokens(q).wait_recv()
        @pl.when(j == 6)
        def _():
            for q in range(M // C, own_rows // C):
                tokens(q).wait_recv()
        @pl.when(j == TURN)
        def _():
            turn().wait_recv()
            for t in range(V0, NF):
                late_send(t).start()
        for at, tiles in SPREAD.items():
            @pl.when(j == at)
            def _():
                for t in tiles:
                    late_send(t).wait_recv()
                for t in tiles:
                    late_across(t, late_rows(t)).start()

        new = pick(NEW, j) == 1
        @pl.when(j == 2)
        def _():
            start_x(rows, slot_x)

        @pl.when(new)
        def _():
            load_x(rows, slot_x)[0].wait()

        @pl.when((load_n >= 0) & (j != 2))
        def _():
            start_x(load_n, 1 - slot_x)

        @pl.when(j == 2)
        def _():
            start_x(pick([JOBS[4][0]], j), 1 - slot_x)

        @pl.when(pick([int(m[0] == "z") for m in modes], j) == 1)
        def _():
            @pl.loop(0, M // R)
            def _(r):
                acc[pl.ds(pl.multiple_of(r * R, R), R)] = jnp.zeros((R, acc.shape[1]), f32)

        @pl.when(pick([int(m[0] == "l") for m in modes], j) == 1)
        def _():
            swap(rows, False).start()
            swap(rows, False).wait()

        for k, at_job in enumerate(FINAL):
            @pl.when(j == at_job)
            def _():
                for q in range(M // C):
                    products(k, q).wait_recv()
                for ref in (x.at[pl.ds(k * M, M)], part.at[k]):
                    copy = pltpu.make_async_copy(ref, xv.at[slot_x], x_load.at[slot_x])
                    copy.start()
                    copy.wait()

                    @pl.loop(0, M // R)
                    def _(r):
                        at = pl.ds(pl.multiple_of(r * R, R), R)
                        acc[at] = acc[at] + xv[slot_x, at].astype(f32)

        def step(i, _):
            f = f0 + i
            slot = (step0 + i) % 2
            ends = i + 1 == n

            @pl.when(jnp.where(i == 0, own_h_before == 1, is_h))
            def _():
                store_h(1 - slot, rows, f)[0].wait()

            @pl.when(first == 1)
            def _():
                for copy in load_first(slot, f, MINE):
                    copy.wait()

            @pl.when(second == 1)
            def _():
                for copy in load_second(slot, f, MINE):
                    copy.wait()

            half_h = (src == LATE) & (f == NF - 1)

            @pl.when((first == 0) & jnp.logical_not(half_h))
            def _():
                load_h(slot, rows, f, YS).wait()

            @pl.when(half_h)
            def _():
                load_h(slot, rows, f, YS, True).wait()

            @pl.when(jnp.logical_not(ends & (j == NJ - 1)))
            def _():
                prefetch(1 - slot, jnp.where(ends, rows_n, rows), jnp.where(ends, src_n, src), jnp.where(ends, f0_n, f + 1),
                         jnp.where(ends, first_n, first), jnp.where(ends, second_n, second), jnp.where(ends, fresh_n, fresh))

            @pl.when(first == 1)
            def _():
                skip = lax.max(f * FT - (ff - FT), 0)
                own = lax.broadcasted_iota(jnp.int32, (MS, FT), 1) >= skip
                for r in range(0, M, MS):
                    at = slice(r, r + MS)
                    a = jnp.dot(xv[slot_x, at], gv[slot], preferred_element_type=f32)
                    b = jnp.dot(xv[slot_x, at], uv[slot], preferred_element_type=f32)
                    hv[slot, at] = jnp.where(own, a * jax.nn.sigmoid(a) * b, 0.0).astype(bf16)

            @pl.when(second == 1)
            def _():
                for c in range(0, acc.shape[1], NC):
                    cols = slice(c, c + NC)
                    acc[:, cols] += jnp.dot(hv[slot], dv[slot, :, cols], preferred_element_type=f32)

            @pl.when(is_h & (rows < N1))
            def _():
                store_h(slot, rows, f)[0].start()

            @pl.when(is_h & (rows >= N1))
            def _():
                store_h(slot, rows, f)[1].start()
            return 0

        lax.fori_loop(0, n, step, 0)

        @pl.when(is_h & (rows >= N1))
        def _():
            store_h((step0 + n - 1) % 2, rows, f0)[1].wait()

            @pl.loop(0, n)
            def _(i):
                @pl.when(f0 + i < NF - 1)
                def _():
                    hidden(rows - 2, f0 + i).start()

                @pl.when(f0 + i == NF - 1)
                def _():
                    hidden(rows - 2, NF - 1, True).start()

        for at, tiles in FORWARD.items():
            @pl.when(j == at)
            def _():
                for t in tiles:
                    late_send(t).start()

        @pl.when(pick([int(m[1] == "s") for m in modes], j) == 1)
        def _():
            swap(rows, True).start()
            swap(rows, True).wait()

        @pl.when(pick([int(m[1] == "r") for m in modes], j) == 1)
        def _():
            for q in range(M // C):
                @pl.loop(0, C // R)
                def _(r):
                    at = pl.ds(pl.multiple_of(q * C + r * R, R), R)
                    xv[slot_x, at] = acc[at].astype(bf16)
                store(rows - 2, q, slot_x).start()
            for q in range(M // C):
                store(rows - 2, q, slot_x).wait()
                products(rows - 2, q).start()

        @pl.when(j == LEAVE)
        def _():
            @pl.loop(0, M // R)
            def _(r):
                at = pl.ds(pl.multiple_of(r * R, R), R)
                xv[0, at] = acc[at].astype(bf16)
        return step0 + n

    lax.fori_loop(0, NJ, job, jnp.int32(0))

    for q in range(own_rows // C):
        tokens(q).wait_send()
    turn().wait_send()
    for t in range(NF):
        for k in range(3):
            along_y(k, t, width_of(t)).wait_send()
            across(k, t, width_of(t)).wait_send()
    for c in range(ff // WC):
        for k in range(3):
            mine(k, c).wait_send()
    for t in range(L0, NF):
        late_send(t).wait_send()
        late_across(t, late_rows(t)).wait_send()
    for k in range(2):
        for q in range(M // C):
            products(k, q).wait_send()
    for rows, src, f0, n, first, second, _ in JOBS:
        if rows >= N1 and not second:
            for t in range(f0, f0 + n):
                hidden(rows - 2, t, t == NF - 1).wait_send()


def write(xv, acc, out, yv, sem):
    step = 128
    early = pltpu.make_async_copy(xv.at[0], out.at[pl.ds(0, M)], sem.at[0])
    early.start()
    late = [pltpu.make_async_copy(yv.at[pl.ds(k * step, step)], out.at[pl.ds(M + k * step, step)], sem.at[1 + k])
            for k in range(M // step)]
    for k, copy in enumerate(late):
        @pl.loop(0, step // R)
        def _(r):
            at = pl.ds(pl.multiple_of(k * step + r * R, R), R)
            yv[at] = acc[at].astype(jnp.bfloat16)
        copy.start()
    early.wait()
    for copy in late:
        copy.wait()


def solution(mesh):
    def body(x, wg, wu, wd):
        r, d = x.shape
        kd, ff = wg.shape
        dc = wd.shape[1]
        bf, f32 = jnp.bfloat16, jnp.float32
        any_ = pl.BlockSpec(memory_space=pl.ANY)
        vmem = pl.BlockSpec(memory_space=pltpu.VMEM)
        nh = (2, NF, M, FT)
        shapes = [(2, M, d), (kd, ff), (kd, ff), (ff, dc), (2, kd, ff), (2, kd, ff), (2, ff, dc),
                  (2, ff - L0 * FT, dc), (ff - V0 * FT, dc), nh, nh, nh]
        dma = pltpu.SemaphoreType.DMA
        nl, nn, nw = NF - L0, r // C, ff // WC
        work = [jax.ShapeDtypeStruct(s, bf) for s in shapes] + [
            jax.ShapeDtypeStruct((2, M, d), f32), jax.ShapeDtypeStruct((2, M, d), bf), jax.ShapeDtypeStruct((2, M, d), bf)]
        xv, acc, *_ = pl.pallas_call(
            kernel,
            out_shape=[pltpu.VMEM((2, M, d), bf), pltpu.VMEM((M, d), f32)] + work,
            in_specs=[any_] * 4,
            out_specs=[vmem] * 2 + [any_] * len(work),
            scratch_shapes=[
                pltpu.VMEM((2, d, FT), bf), pltpu.VMEM((2, d, FT), bf), pltpu.VMEM((2, FT, d), bf),
                pltpu.VMEM((2, M, FT), bf),
                dma((3, NF)), dma((3, NF)), dma((3, NF)), dma((3, NF)), dma((3, nw)), dma((3, nw)),
                dma((nl,)), dma((nl,)), dma((nl,)), dma((nl,)), dma((nn,)), dma((nn,)),
                dma((2, M // C)), dma((2, M // C)), dma((2, NF)), dma((2, NF)), dma((2,)),
                dma((2, 7)), dma((2,)), dma, dma((2,)), dma((M // C,)),
            ],
            compiler_params=pltpu.CompilerParams(collective_id=0, has_side_effects=True, vmem_limit_bytes=23 * 2**20),
        )(x, wg, wu, wd)
        return pl.pallas_call(
            write,
            out_shape=jax.ShapeDtypeStruct((r, d), bf),
            in_specs=[vmem] * 2,
            out_specs=any_,
            scratch_shapes=[pltpu.VMEM((M, d), bf), dma((9,))],
            compiler_params=pltpu.CompilerParams(vmem_limit_bytes=12 * 2**20),
        )(xv, acc)

    return jax.shard_map(body, mesh=mesh, in_specs=(P(("dp", "tp"), None), P("dp", "tp"), P("dp", "tp"), P("tp", "dp")), out_specs=P(("dp", "tp"), None), check_vma=False)
```

time: 3750 us -> 1300 us (0.35)
  waiting for transfers between devices: 2340 us -> 0 us
  Pallas kernels: 0 us -> 1280 us
  matrix products: 946 us -> 0 us
  local copies, waits for them, and re-layouts: 199 us -> 14.5 us
  blocking collectives: 159 us -> 0 us
  other arithmetic: 76.1 us -> 0 us
    unnamed x8 -> x0, waiting for transfers between devices: 1480 us -> none
    pallas_call x0 -> x2, Pallas kernels: none -> 1280 us  [the longest x1 1270 us: body(): pl.pallas_call(kernel, out_shape=[pltpu.VMEM((2, M, d), bf), pltpu.VMEM((...]
    dot_general x3 -> x0, matrix products: 946 us -> none  [the longest x1 316 us: body(): jnp.dot(xc, wu, preferred_element_type=jnp.float32).astype(jnp.bfloat16)]
    all_gather x2 -> x0, waiting for transfers between devices: 864 us -> none  [the longest x1 714 us: body(): xt = lax.all_gather(x, 'tp', axis=0, tiled=True)]
    all_to_all x2 -> x0, blocking collectives: 159 us -> none  [the longest x1 137 us: body(): xc = lax.all_to_all(xt, 'dp', 1, 0, tiled=True)]
    all_to_all x1 -> x0, local copies, waits for them, and re-layouts: 98.5 us -> none  [body(): xc = lax.all_to_all(xt, 'dp', 1, 0, tiled=True)]
    convert_element_type x2 -> x0, other arithmetic: 76.1 us -> none  [the longest x1 55.9 us: body(): h = (jax.nn.silu(a) * b).astype(jnp.bfloat16)]
  transfers between devices with their start and end apart: 5 -> 0, of which waited for: 4 -> 0; matrix products, arithmetic and copies ran while one was open for 8% -> 0% of each run, Pallas kernels for 0% -> 0%
where the time goes in v3:
time: 1300 us; the launch traced here: 1290 us
  Pallas kernels  1280 us (98%)
  local copies, waits for them, and re-layouts  14.5 us (1%)
    pallas_call x1, Pallas kernels, body(): pl.pallas_call(kernel, out_shape=[pltpu.VMEM((2, M, d), bf), pltpu.VMEM((...  1270 us

profile of v3, /device:TPU:0, one launch (start us, length us, event | category | flops | bytes accessed | tf_op | source)
XLA Modules:
  0.0 1294.9 jit_solution(18145451752643190541)
XLA Ops:
  0.0 1273.1 %shard_map.46 = (bf16[2,1024,5120]{2,1,0:T(8,128)(2,1)S(1)}, f32[1024,5120]{1,0:T(8,128)S(1)}, bf16[2,1024,5120]{2,1,0:T(8,128)(2,1)}, bf16[2560,3456]{1,0:T(8,1...) custom-call(bf16[2048,5120]{1,0:T(8,128)(2,1)} %x.1, ...), custom_call_target="tpu_custom_call" | custom-call | tf_op jit(solution)/shard_map/pallas_call | solution.py:553
  1273.1 0.0 copy-start
  1273.1 7.5 copy-done
  1280.6 0.0 copy-start.1
  1280.6 7.0 copy-done.1
  1287.6 7.3 shard_map.47
Async XLA Ops:
  1273.1 7.5 copy-start
  1280.6 7.0 copy-start.1

commit v4 on v3

--- a/solution.py
+++ b/solution.py
@@ -15,7 +15,8 @@
 MS = 512
 R = 32
 L0 = 6
-V0 = 11
+TURN_ROW = 2688
+PIECES = ((1536, 256), (1792, 256), (2048, 256), (2304, 256), (2560, 128), (2688, 128), (2816, 256), (3072, 256), (3328, 128))
 
 O1, O2, N1, N2 = range(4)
 MINE, YS, LATE = range(3)
@@ -42,31 +43,44 @@
     (N1, YS, 10, 1, 1, 0, "k-"),
     (O1, YS, 10, 1, 1, 0, "k-"),
     (O2, YS, 10, 1, 1, 0, "k-"),
+    (N2, YS, 10, 1, 1, 0, "k-"),
     (O1, YS, 8, 3, 0, 1, "l-"),
     (O1, LATE, 6, 2, 0, 1, "ks"),
     (N1, YS, 11, 1, 1, 0, "k-"),
     (O1, YS, 11, 1, 1, 0, "k-"),
     (O2, YS, 11, 1, 1, 0, "k-"),
-    (O2, YS, 8, 4, 0, 1, "ls"),
+    (N2, YS, 11, 1, 1, 0, "k-"),
+    (O2, YS, 8, 4, 0, 1, "lh"),
     (N1, YS, 12, 1, 1, 0, "k-"),
+    (N2, YS, 12, 1, 1, 0, "k-"),
     (O1, YS, 12, 1, 1, 0, "k-"),
     (O2, YS, 12, 1, 1, 0, "k-"),
+    (O1, YS, 11, 2, 0, 1, "l-"),
+    (N2, YS, 13, 1, 1, 0, "k-"),
     (N1, YS, 13, 1, 1, 0, "k-"),
-    (N2, YS, 10, 4, 1, 0, "k-"),
     (O1, YS, 13, 1, 1, 0, "k-"),
     (O2, YS, 13, 1, 1, 0, "k-"),
-    (O1, YS, 11, 3, 0, 1, "l-"),
-    (O1, LATE, 8, 6, 0, 1, "k-"),
-    (O2, YS, 12, 2, 0, 1, "l-"),
-    (O2, LATE, 9, 5, 0, 1, "k-"),
+    (O1, YS, 13, 1, 0, 1, "k-"),
+    (O1, LATE, 8, 2, 0, 1, "k-"),
+    (O1, LATE, 10, 2, 0, 1, "kv"),
+    (O2, YS, 12, 2, 0, 1, "h-"),
+    (O2, LATE, 9, 3, 0, 1, "k-"),
+    (O2, LATE, 12, 1, 0, 1, "k-"),
+    (O2, LATE, 13, 1, 0, 1, "k-"),
+    (O1, LATE, 12, 2, 0, 1, "v-"),
 )
 NJ = len(JOBS)
 AHEAD = {2: (0, 1), 3: (2, 3), 8: (6,)}
-FORWARD = {9: (6, 7), 15: (8, 9), 19: (10,)}
+FORWARD = {9: (0, 1), 15: (2, 3), 19: (4,)}
+SENDS = {9: ((0, 6), (0, 7)), 15: ((0, 8), (0, 9)), 16: ((1, 9),), 19: ((0, 10),), 25: ((0, 11),), 28: ((1, 10), (1, 11)),
+         31: ((1, 12),), 35: ((1, 13),), 36: ((0, 12), (0, 13))}
 TURN = 8
-SPREAD = {17: (6, 7), 32: (8, 9), 36: (10, 11, 12, 13)}
-FINAL = (22, 27)
-LEAVE = 36
+SPREAD = {17: (0, 1), 35: (2, 3), 40: (4, 5, 6), 43: (7,), 44: (8,)}
+FINAL = (23, 29)
+FETCH = 39
+LEAVE = 45
+PATIENT = (43, 44, 45)
+SECOND = 12
 
 
 def plan():
@@ -93,8 +107,13 @@
 SLOT, NEW, LOAD, FRESH = plan()
 
 
-def kernel(x, wg, wu, wd, xv, acc, gn, pg, pu, pd, yg, yu, yd, ld, xd, ho, hs, hr, sv, prod, part,
-           gv, uv, dv, hv,
+def spot(b, gv, uv):
+    per = gv.shape[1] // M
+    return (gv, uv)[b // (2 * per)], b // per % 2, b % per * M
+
+
+def kernel(x, wg, wu, wd, gv, uv, acc, gn, pg, pu, pd, yg, yu, yd, ld, xd, ho, hs, hr, sv, sh, prod, part,
+           xv, dv, hv,
            y_send, y_recv, d_send, d_recv, w_send, w_recv, l_send, l_recv, e_send, e_recv, n_send, n_recv,
            r_send, r_recv, h_send, h_recv, t_sem, w_load, x_load, s_sem, h_sem, o_sem):
     tp, dp = lax.axis_index("tp"), lax.axis_index("dp")
@@ -151,19 +170,20 @@
     def width_of(t):
         return ff - last if t == NF - 1 else FT
 
-    def late_rows(t):
-        return pl.ds(col(t - L0), width_of(t) if isinstance(t, int) else FT)
-
-    def late_send(t):
-        if t < V0:
-            return remote(yd.at[0, pl.ds(col(t), FT)], ld.at[0, late_rows(t)], l_send.at[t - L0], l_recv.at[t - L0], to_x)
-        return remote(xd.at[pl.ds(col(t - V0), width_of(t))], ld.at[0, late_rows(t)], l_send.at[t - L0], l_recv.at[t - L0], to_y)
-
-    def late_across(t, rows):
-        return remote(ld.at[0, rows], ld.at[1, rows], e_send.at[t - L0], e_recv.at[t - L0], to_core)
+    def late_send(p):
+        row, n = PIECES[p]
+        dst = ld.at[0, pl.ds(row - L0 * FT, n)]
+        if row < TURN_ROW:
+            return remote(yd.at[0, pl.ds(row, n)], dst, l_send.at[p], l_recv.at[p], to_x)
+        return remote(xd.at[pl.ds(row - TURN_ROW, n)], dst, l_send.at[p], l_recv.at[p], to_y)
+
+    def late_across(p):
+        row, n = PIECES[p]
+        at = pl.ds(row - L0 * FT, n)
+        return remote(ld.at[0, at], ld.at[1, at], e_send.at[p], e_recv.at[p], to_core)
 
     def turn():
-        return remote(wd.at[pl.ds(V0 * FT, ff - V0 * FT)], xd, t_sem.at[0], t_sem.at[1], to_x)
+        return remote(wd.at[pl.ds(TURN_ROW, ff - TURN_ROW)], xd, t_sem.at[0], t_sem.at[1], to_x)
 
     def hidden(k, t, end=False):
         at = (k, t, slice(None), pl.ds(NF * FT - ff, ff - last)) if end else (k, t)
@@ -268,13 +288,12 @@
             hv[slot, :, pl.ds(0, NF * FT - ff)] = jnp.zeros((M, NF * FT - ff), bf16)
             load_h(slot, rows, NF - 1, LATE, True).start()
 
-        @pl.when((src == LATE) & (rows == O1) & (f < NF - 1))
-        def _():
-            late_across(f, late_rows(f)).wait_recv()
-
-        @pl.when((src == LATE) & (rows == O1) & (f == NF - 1))
-        def _():
-            late_across(NF - 1, late_rows(NF - 1)).wait_recv()
+        for t in range(L0, NF):
+            @pl.when((src == LATE) & (rows == (O1 if t < SECOND else O2)) & (f == t))
+            def _():
+                for p, (row, _) in enumerate(PIECES):
+                    if row // FT == t:
+                        late_across(p).wait_recv()
 
         for value in (MINE, YS):
             @pl.when((first == 1) & (src == value))
@@ -314,6 +333,9 @@
         rows_n, src_n, f0_n, _, first_n, second_n = [pick(c, after) for c in columns]
         fresh, fresh_n = pick(FRESH, j), pick(FRESH, after)
         slot_x = pick(SLOT, j)
+
+        def is_mode(at, what):
+            return pick([int(m[at] == what) for m in modes], j) == 1
         load_n = pick(LOAD, j)
         is_h = (first == 1) & (second == 0)
         before = lax.max(j - 1, 0)
@@ -335,15 +357,16 @@
         @pl.when(j == TURN)
         def _():
             turn().wait_recv()
-            for t in range(V0, NF):
-                late_send(t).start()
-        for at, tiles in SPREAD.items():
+            for p, (row, _) in enumerate(PIECES):
+                if row >= TURN_ROW:
+                    late_send(p).start()
+        for at, ps in SPREAD.items():
             @pl.when(j == at)
             def _():
-                for t in tiles:
-                    late_send(t).wait_recv()
-                for t in tiles:
-                    late_across(t, late_rows(t)).start()
+                for p in ps:
+                    late_send(p).wait_recv()
+                for p in ps:
+                    late_across(p).start()
 
         new = pick(NEW, j) == 1
         @pl.when(j == 2)
@@ -362,16 +385,41 @@
         def _():
             start_x(pick([JOBS[4][0]], j), 1 - slot_x)
 
-        @pl.when(pick([int(m[0] == "z") for m in modes], j) == 1)
+        @pl.when(is_mode(0, "z"))
         def _():
             @pl.loop(0, M // R)
             def _(r):
                 acc[pl.ds(pl.multiple_of(r * R, R), R)] = jnp.zeros((R, acc.shape[1]), f32)
 
-        @pl.when(pick([int(m[0] == "l") for m in modes], j) == 1)
+        @pl.when(is_mode(0, "l"))
         def _():
             swap(rows, False).start()
             swap(rows, False).wait()
+
+        def to_rows(slot):
+            @pl.loop(0, M // R)
+            def _(r):
+                at = pl.ds(pl.multiple_of(r * R, R), R)
+                xv[slot, at] = acc[at].astype(bf16)
+
+        def from_rows(slot):
+            @pl.loop(0, M // R)
+            def _(r):
+                at = pl.ds(pl.multiple_of(r * R, R), R)
+                acc[at] = xv[slot, at].astype(f32)
+
+        @pl.when(j == FETCH)
+        def _():
+            pltpu.make_async_copy(sh, xv.at[1], x_load.at[1]).start()
+
+        @pl.when(is_mode(0, "h"))
+        def _():
+            pltpu.make_async_copy(sh, xv.at[1], x_load.at[1]).wait()
+            from_rows(1)
+
+        @pl.when(is_mode(0, "v"))
+        def _():
+            from_rows(0)
 
         for k, at_job in enumerate(FINAL):
             @pl.when(j == at_job)
@@ -417,10 +465,12 @@
             def _():
                 load_h(slot, rows, f, YS, True).wait()
 
-            @pl.when(jnp.logical_not(ends & (j == NJ - 1)))
-            def _():
+            def load_next():
                 prefetch(1 - slot, jnp.where(ends, rows_n, rows), jnp.where(ends, src_n, src), jnp.where(ends, f0_n, f + 1),
                          jnp.where(ends, first_n, first), jnp.where(ends, second_n, second), jnp.where(ends, fresh_n, fresh))
+
+            patient = (j >= PATIENT[0]) & (j <= PATIENT[-1])
+            pl.when(jnp.logical_not(patient | (ends & (j == NJ - 1))))(load_next)
 
             @pl.when(first == 1)
             def _():
@@ -438,6 +488,8 @@
                     cols = slice(c, c + NC)
                     acc[:, cols] += jnp.dot(hv[slot], dv[slot, :, cols], preferred_element_type=f32)
 
+            pl.when(patient)(load_next)
+
             @pl.when(is_h & (rows < N1))
             def _():
                 store_h(slot, rows, f)[0].start()
@@ -453,28 +505,35 @@
         def _():
             store_h((step0 + n - 1) % 2, rows, f0)[1].wait()
 
-            @pl.loop(0, n)
-            def _(i):
-                @pl.when(f0 + i < NF - 1)
-                def _():
-                    hidden(rows - 2, f0 + i).start()
-
-                @pl.when(f0 + i == NF - 1)
-                def _():
-                    hidden(rows - 2, NF - 1, True).start()
-
-        for at, tiles in FORWARD.items():
+        for at, pairs in SENDS.items():
             @pl.when(j == at)
             def _():
-                for t in tiles:
-                    late_send(t).start()
-
-        @pl.when(pick([int(m[1] == "s") for m in modes], j) == 1)
+                for k, t in pairs:
+                    hidden(k, t, t == NF - 1).start()
+
+        for at, ps in FORWARD.items():
+            @pl.when(j == at)
+            def _():
+                for p in ps:
+                    late_send(p).start()
+
+        @pl.when(is_mode(1, "s"))
         def _():
             swap(rows, True).start()
             swap(rows, True).wait()
 
-        @pl.when(pick([int(m[1] == "r") for m in modes], j) == 1)
+        @pl.when(is_mode(1, "h"))
+        def _():
+            to_rows(slot_x)
+            copy = pltpu.make_async_copy(xv.at[slot_x], sh, s_sem)
+            copy.start()
+            copy.wait()
+
+        @pl.when(is_mode(1, "v"))
+        def _():
+            to_rows(0)
+
+        @pl.when(is_mode(1, "r"))
         def _():
             for q in range(M // C):
                 @pl.loop(0, C // R)
@@ -490,8 +549,10 @@
         def _():
             @pl.loop(0, M // R)
             def _(r):
-                at = pl.ds(pl.multiple_of(r * R, R), R)
-                xv[0, at] = acc[at].astype(bf16)
+                for b in range(acc.shape[1] // FT):
+                    buf, k, row = spot(b, gv, uv)
+                    at = pl.ds(pl.multiple_of(r * R, R), R)
+                    buf[k, pl.ds(pl.multiple_of(row + r * R, R), R)] = acc[at, b * FT:(b + 1) * FT].astype(bf16)
         return step0 + n
 
     lax.fori_loop(0, NJ, job, jnp.int32(0))
@@ -506,32 +567,34 @@
     for c in range(ff // WC):
         for k in range(3):
             mine(k, c).wait_send()
-    for t in range(L0, NF):
-        late_send(t).wait_send()
-        late_across(t, late_rows(t)).wait_send()
+    for p in range(len(PIECES)):
+        late_send(p).wait_send()
+        late_across(p).wait_send()
     for k in range(2):
         for q in range(M // C):
             products(k, q).wait_send()
-    for rows, src, f0, n, first, second, _ in JOBS:
-        if rows >= N1 and not second:
-            for t in range(f0, f0 + n):
-                hidden(rows - 2, t, t == NF - 1).wait_send()
-
-
-def write(xv, acc, out, yv, sem):
+    for pairs in SENDS.values():
+        for k, t in pairs:
+            hidden(k, t, t == NF - 1).wait_send()
+
+
+def write(gv, uv, acc, out, yv, sem):
     step = 128
-    early = pltpu.make_async_copy(xv.at[0], out.at[pl.ds(0, M)], sem.at[0])
-    early.start()
-    late = [pltpu.make_async_copy(yv.at[pl.ds(k * step, step)], out.at[pl.ds(M + k * step, step)], sem.at[1 + k])
-            for k in range(M // step)]
+    early, late = [], []
+    for b in range(out.shape[1] // FT):
+        buf, k, row = spot(b, gv, uv)
+        early.append(pltpu.make_async_copy(buf.at[k, pl.ds(row, M)], out.at[pl.ds(M, M), pl.ds(b * FT, FT)], sem.at[b]))
+    for k in range(M // step):
+        late.append(pltpu.make_async_copy(yv.at[pl.ds(k * step, step)], out.at[pl.ds(k * step, step)], sem.at[len(early) + k]))
+    for copy in early:
+        copy.start()
     for k, copy in enumerate(late):
         @pl.loop(0, step // R)
         def _(r):
             at = pl.ds(pl.multiple_of(k * step + r * R, R), R)
             yv[at] = acc[at].astype(jnp.bfloat16)
         copy.start()
-    early.wait()
-    for copy in late:
+    for copy in early + late:
         copy.wait()
 
 
@@ -545,33 +608,32 @@
         vmem = pl.BlockSpec(memory_space=pltpu.VMEM)
         nh = (2, NF, M, FT)
         shapes = [(2, M, d), (kd, ff), (kd, ff), (ff, dc), (2, kd, ff), (2, kd, ff), (2, ff, dc),
-                  (2, ff - L0 * FT, dc), (ff - V0 * FT, dc), nh, nh, nh]
+                  (2, ff - L0 * FT, dc), (ff - TURN_ROW, dc), nh, nh, nh]
         dma = pltpu.SemaphoreType.DMA
-        nl, nn, nw = NF - L0, r // C, ff // WC
+        nl, nn, nw = len(PIECES), r // C, ff // WC
         work = [jax.ShapeDtypeStruct(s, bf) for s in shapes] + [
-            jax.ShapeDtypeStruct((2, M, d), f32), jax.ShapeDtypeStruct((2, M, d), bf), jax.ShapeDtypeStruct((2, M, d), bf)]
-        xv, acc, *_ = pl.pallas_call(
+            jax.ShapeDtypeStruct((2, M, d), f32), jax.ShapeDtypeStruct((M, d), bf), jax.ShapeDtypeStruct((2, M, d), bf), jax.ShapeDtypeStruct((2, M, d), bf)]
+        gv, uv, acc, *_ = pl.pallas_call(
             kernel,
-            out_shape=[pltpu.VMEM((2, M, d), bf), pltpu.VMEM((M, d), f32)] + work,
+            out_shape=[pltpu.VMEM((2, d, FT), bf)] * 2 + [pltpu.VMEM((M, d), f32)] + work,
             in_specs=[any_] * 4,
-            out_specs=[vmem] * 2 + [any_] * len(work),
+            out_specs=[vmem] * 3 + [any_] * len(work),
             scratch_shapes=[
-                pltpu.VMEM((2, d, FT), bf), pltpu.VMEM((2, d, FT), bf), pltpu.VMEM((2, FT, d), bf),
-                pltpu.VMEM((2, M, FT), bf),
+                pltpu.VMEM((2, M, d), bf), pltpu.VMEM((2, FT, d), bf), pltpu.VMEM((2, M, FT), bf),
                 dma((3, NF)), dma((3, NF)), dma((3, NF)), dma((3, NF)), dma((3, nw)), dma((3, nw)),
                 dma((nl,)), dma((nl,)), dma((nl,)), dma((nl,)), dma((nn,)), dma((nn,)),
                 dma((2, M // C)), dma((2, M // C)), dma((2, NF)), dma((2, NF)), dma((2,)),
                 dma((2, 7)), dma((2,)), dma, dma((2,)), dma((M // C,)),
             ],
-            compiler_params=pltpu.CompilerParams(collective_id=0, has_side_effects=True, vmem_limit_bytes=23 * 2**20),
+            compiler_params=pltpu.CompilerParams(collective_id=0, has_side_effects=True, vmem_limit_bytes=int(33.9 * 2**20)),
         )(x, wg, wu, wd)
         return pl.pallas_call(
             write,
             out_shape=jax.ShapeDtypeStruct((r, d), bf),
-            in_specs=[vmem] * 2,
+            in_specs=[vmem] * 3,
             out_specs=any_,
-            scratch_shapes=[pltpu.VMEM((M, d), bf), dma((9,))],
+            scratch_shapes=[pltpu.VMEM((M, d), bf), dma((28,))],
             compiler_params=pltpu.CompilerParams(vmem_limit_bytes=12 * 2**20),
-        )(xv, acc)
+        )(gv, uv, acc)
 
     return jax.shard_map(body, mesh=mesh, in_specs=(P(("dp", "tp"), None), P("dp", "tp"), P("dp", "tp"), P("tp", "dp")), out_specs=P(("dp", "tp"), None), check_vma=False)

time: 1300 us -> 1280 us (0.985)
  local copies, waits for them, and re-layouts: 14.5 us -> 0 us
    unnamed x4 -> x0, local copies, waits for them, and re-layouts: 14.5 us -> none
where the time goes in v4:
time: 1280 us
  Pallas kernels  1280 us (100%)
    pallas_call x1, Pallas kernels, body(): pl.pallas_call(kernel, out_shape=[pltpu.VMEM((2, d, FT), bf)] * 2 + [pltp...  1270 us

profile of v4, /device:TPU:0, one launch (start us, length us, event | category | flops | bytes accessed | tf_op | source)
XLA Modules:
  0.0 1281.7 jit_solution(9164875673289240247)
XLA Ops:
  0.0 1274.3 %shard_map.46 = (bf16[2,5120,256]{2,1,0:T(8,128)(2,1)S(1)}, bf16[2,5120,256]{2,1,0:T(8,128)(2,1)S(1)}, f32[1024,5120]{1,0:T(8,128)S(1)}, bf16[2,1024,5120]{2,1,0...) custom-call(bf16[2048,5120]{1,0:T(8,128)(2,1)} %x.1, ...), custom_call_target="tpu_custom_call" | custom-call | tf_op jit(solution)/shard_map/pallas_call | solution.py:616
  1274.3 7.3 shard_map.47

commit v5 on v4

--- a/solution.py
+++ b/solution.py
@@ -20,55 +20,17 @@
 
 O1, O2, N1, N2 = range(4)
 MINE, YS, LATE = range(3)
-JOBS = (
-    (O1, MINE, 0, 14, 1, 1, "zs"),
-    (O2, MINE, 0, 14, 1, 1, "zs"),
-    (N1, MINE, 0, 14, 1, 1, "z-"),
-    (N1, YS, 0, 5, 1, 1, "k-"),
-    (O1, YS, 0, 5, 1, 0, "k-"),
-    (O2, YS, 0, 5, 1, 0, "k-"),
-    (N1, YS, 5, 1, 1, 1, "kr"),
-    (N2, MINE, 0, 14, 1, 1, "z-"),
-    (N2, YS, 0, 7, 1, 1, "k-"),
-    (N1, YS, 6, 2, 1, 0, "k-"),
-    (O1, YS, 5, 3, 1, 0, "k-"),
-    (O2, YS, 5, 3, 1, 0, "k-"),
-    (N2, YS, 7, 2, 1, 1, "kr"),
-    (O1, YS, 0, 8, 0, 1, "ls"),
-    (O2, YS, 0, 8, 0, 1, "ls"),
-    (N1, YS, 8, 2, 1, 0, "k-"),
-    (N2, YS, 9, 1, 1, 0, "k-"),
-    (O1, YS, 8, 2, 1, 0, "k-"),
-    (O2, YS, 8, 2, 1, 0, "k-"),
-    (N1, YS, 10, 1, 1, 0, "k-"),
-    (O1, YS, 10, 1, 1, 0, "k-"),
-    (O2, YS, 10, 1, 1, 0, "k-"),
-    (N2, YS, 10, 1, 1, 0, "k-"),
-    (O1, YS, 8, 3, 0, 1, "l-"),
-    (O1, LATE, 6, 2, 0, 1, "ks"),
-    (N1, YS, 11, 1, 1, 0, "k-"),
-    (O1, YS, 11, 1, 1, 0, "k-"),
-    (O2, YS, 11, 1, 1, 0, "k-"),
-    (N2, YS, 11, 1, 1, 0, "k-"),
-    (O2, YS, 8, 4, 0, 1, "lh"),
-    (N1, YS, 12, 1, 1, 0, "k-"),
-    (N2, YS, 12, 1, 1, 0, "k-"),
-    (O1, YS, 12, 1, 1, 0, "k-"),
-    (O2, YS, 12, 1, 1, 0, "k-"),
-    (O1, YS, 11, 2, 0, 1, "l-"),
-    (N2, YS, 13, 1, 1, 0, "k-"),
-    (N1, YS, 13, 1, 1, 0, "k-"),
-    (O1, YS, 13, 1, 1, 0, "k-"),
-    (O2, YS, 13, 1, 1, 0, "k-"),
-    (O1, YS, 13, 1, 0, 1, "k-"),
-    (O1, LATE, 8, 2, 0, 1, "k-"),
-    (O1, LATE, 10, 2, 0, 1, "kv"),
-    (O2, YS, 12, 2, 0, 1, "h-"),
-    (O2, LATE, 9, 3, 0, 1, "k-"),
-    (O2, LATE, 12, 1, 0, 1, "k-"),
-    (O2, LATE, 13, 1, 0, 1, "k-"),
-    (O1, LATE, 12, 2, 0, 1, "v-"),
+ORDER = (
+    "O1M0014Bzs", "O2M0014Bzs", "N1M0014Bz-", "N1Y0005Bk-", "O1Y0005Fk-", "O2Y0005Fk-", "N1Y0501Bkr",
+    "N2M0014Bz-", "N2Y0007Bk-", "N1Y0602Fk-", "O1Y0503Fk-", "O2Y0503Fk-", "N2Y0702Bkr", "O1Y0008Sls",
+    "O2Y0008Sls", "N1Y0802Fk-", "N2Y0901Fk-", "O1Y0802Fk-", "O2Y0802Fk-", "N1Y1001Fk-", "O1Y1001Fk-",
+    "O2Y1001Fk-", "N2Y1001Fk-", "O1Y0803Sl-", "O1L0602Sks", "N1Y1101Fk-", "O1Y1101Fk-", "O2Y1101Fk-",
+    "N2Y1101Fk-", "O2Y0804Slh", "N1Y1201Fk-", "N2Y1201Fk-", "O1Y1201Fk-", "O2Y1201Fk-", "O1Y1102Sl-",
+    "N2Y1301Fk-", "N1Y1301Fk-", "O1Y1301Fk-", "O2Y1301Fk-", "O1Y1301Sk-", "O1L0802Sk-", "O1L1002Skv",
+    "O2Y1202Sh-", "O2L0903Sk-", "O2L1201Sk-", "O2L1301Sk-", "O1-0001Nk-", "O1L1202Sv-",
 )
+JOBS = tuple((("O1", "O2", "N1", "N2").index(o[:2]), "MYL-".index(o[2]), int(o[3:5]), int(o[5:7]), int(o[7] in "BF"), int(o[7] in "BS"), o[8:])
+             for o in ORDER)
 NJ = len(JOBS)
 AHEAD = {2: (0, 1), 3: (2, 3), 8: (6,)}
 FORWARD = {9: (0, 1), 15: (2, 3), 19: (4,)}
@@ -79,7 +41,6 @@
 FINAL = (23, 29)
 FETCH = 39
 LEAVE = 45
-PATIENT = (43, 44, 45)
 SECOND = 12
 
 
@@ -105,6 +66,24 @@
 
 
 SLOT, NEW, LOAD, FRESH = plan()
+FIELDS = (("rows", 4), ("src", 4), ("f0", 16), ("n", 16), ("first", 2), ("second", 2), ("slot", 2), ("new", 2), ("load", 8),
+          ("fresh", 16), ("before", 8), ("after", 8))
+
+
+def packed(j):
+    rows, src, f0, n, first, second, (before, after) = JOBS[j]
+    values = (rows, src, f0, n, first, second, SLOT[j], NEW[j], LOAD[j] + 1, FRESH[j], "kzlhv".index(before), "-srhv".index(after))
+    word, scale = 0, 1
+    for value, (_, size) in zip(values, FIELDS):
+        word, scale = word + value * scale, scale * size
+    return word
+
+
+def unpack(word):
+    got = {}
+    for name, size in FIELDS:
+        got[name], word = lax.rem(word, size), lax.div(word, size)
+    return got
 
 
 def spot(b, gv, uv):
@@ -142,6 +121,9 @@
                 got = jnp.where(j == k, v, got)
         return got
 
+    def once(cond):
+        return lambda fn: lax.fori_loop(0, jnp.where(cond, 1, 0), lambda _, c: (fn(), c)[1], 0)
+
     def col(t):
         return t * FT if isinstance(t, int) else pl.multiple_of(t * FT, FT)
 
@@ -249,66 +231,77 @@
             across(k, t, width_of(t)).start()
 
     def prefetch(slot, rows, src, f, first, second, fresh):
-        @pl.when((src == MINE) & (rows == O1) & (f % 3 != 2) & (f < NF - 1))
-        def _():
-            for k in range(3):
-                mine(k, (2 * f + 2) // 3).wait_recv()
-
-        is_new = (src == YS) & (first == 1) & (f >= fresh)
-        early = [t for ts in AHEAD.values() for t in ts]
-        to_send = is_new
-        for t in early:
-            to_send = to_send & (f != t)
-
-        @pl.when(to_send & (f < NF - 1))
-        def _():
-            for k in range(3):
-                along_y(k, f).wait_recv()
-            for k in range(3):
-                across(k, f).start()
-
-        @pl.when(is_new & (f < NF - 1))
-        def _():
-            for k in range(3):
-                across(k, f).wait_recv()
-
-        @pl.when(is_new & (f == NF - 1))
-        def _():
-            send_across(NF - 1)
-            for k in range(3):
-                across(k, NF - 1, width_of(NF - 1)).wait_recv()
-
-        @pl.when((src == LATE) & (f < NF - 1))
-        def _():
-            hidden(rows, f).wait_recv()
-
-        @pl.when((src == LATE) & (f == NF - 1))
-        def _():
-            hidden(rows, NF - 1, True).wait_recv()
-            hv[slot, :, pl.ds(0, NF * FT - ff)] = jnp.zeros((M, NF * FT - ff), bf16)
-            load_h(slot, rows, NF - 1, LATE, True).start()
-
-        for t in range(L0, NF):
-            @pl.when((src == LATE) & (rows == (O1 if t < SECOND else O2)) & (f == t))
-            def _():
-                for p, (row, _) in enumerate(PIECES):
-                    if row // FT == t:
-                        late_across(p).wait_recv()
-
-        for value in (MINE, YS):
-            @pl.when((first == 1) & (src == value))
-            def _():
-                for copy in load_first(slot, f, value):
+        def start(*groups):
+            for copies in groups:
+                for copy in copies:
                     copy.start()
-        for value in (MINE, YS, LATE):
-            @pl.when((second == 1) & (src == value))
-            def _():
-                for copy in load_second(slot, f, value):
-                    copy.start()
-        for value in (YS, LATE):
-            @pl.when((first == 0) & (src == value) & ((src == YS) | (f < NF - 1)))
-            def _():
-                load_h(slot, rows, f, value).start()
+
+        @once(src == MINE)
+        def _():
+            @pl.when((rows == O1) & (f % 3 != 2) & (f < NF - 1))
+            def _():
+                for k in range(3):
+                    mine(k, (2 * f + 2) // 3).wait_recv()
+            start(load_first(slot, f, MINE), load_second(slot, f, MINE))
+
+        @once(src == YS)
+        def _():
+            @once((first == 1) & (f >= fresh))
+            def _():
+                early = [t for ts in AHEAD.values() for t in ts]
+                to_send = f < NF - 1
+                for t in early:
+                    to_send = to_send & (f != t)
+
+                @pl.when(to_send)
+                def _():
+                    for k in range(3):
+                        along_y(k, f).wait_recv()
+                    for k in range(3):
+                        across(k, f).start()
+
+                @pl.when(f < NF - 1)
+                def _():
+                    for k in range(3):
+                        across(k, f).wait_recv()
+
+                @pl.when(f == NF - 1)
+                def _():
+                    send_across(NF - 1)
+                    for k in range(3):
+                        across(k, NF - 1, width_of(NF - 1)).wait_recv()
+
+            @pl.when(first == 1)
+            def _():
+                start(load_first(slot, f, YS))
+
+            @pl.when(first == 0)
+            def _():
+                load_h(slot, rows, f, YS).start()
+
+            @pl.when(second == 1)
+            def _():
+                start(load_second(slot, f, YS))
+
+        @once(src == LATE)
+        def _():
+            @pl.when(f < NF - 1)
+            def _():
+                hidden(rows, f).wait_recv()
+                load_h(slot, rows, f, LATE).start()
+
+            @pl.when(f == NF - 1)
+            def _():
+                hidden(rows, NF - 1, True).wait_recv()
+                hv[slot, :, pl.ds(0, NF * FT - ff)] = jnp.zeros((M, NF * FT - ff), bf16)
+                load_h(slot, rows, NF - 1, LATE, True).start()
+            for t in range(L0, NF):
+                @pl.when((rows == (O1 if t < SECOND else O2)) & (f == t))
+                def _():
+                    for p, (row, _) in enumerate(PIECES):
+                        if row // FT == t:
+                            late_across(p).wait_recv()
+            start(load_second(slot, f, LATE))
 
     def store_h(slot, rows, f):
         return (pltpu.make_async_copy(hv.at[slot], ho.at[lax.min(rows, 1), f], h_sem.at[slot]),
@@ -324,52 +317,49 @@
     start_x(jnp.int32(O1), 0)
     prefetch(0, jnp.int32(O1), jnp.int32(MINE), jnp.int32(0), jnp.int32(1), jnp.int32(1), jnp.int32(NF))
 
-    columns = [[job[i] for job in JOBS] for i in range(6)]
-    modes = [job[6] for job in JOBS]
-
-    def job(j, step0):
-        rows, src, f0, n, first, second = [pick(c, j) for c in columns]
-        after = lax.min(j + 1, NJ - 1)
-        rows_n, src_n, f0_n, _, first_n, second_n = [pick(c, after) for c in columns]
-        fresh, fresh_n = pick(FRESH, j), pick(FRESH, after)
-        slot_x = pick(SLOT, j)
+    words = [packed(j) for j in range(NJ)]
+
+    def job(j, carry):
+        step0, word, own_h_before = carry
+        this = unpack(word)
+        rows, src, f0, n, first, second = (this[k] for k in ("rows", "src", "f0", "n", "first", "second"))
+        word_n = pick(words[1:] + words[-1:], j)
+        nxt = unpack(word_n)
+        fresh, slot_x, load_n = this["fresh"], this["slot"], this["load"] - 1
+        is_h = (first == 1) & (second == 0)
 
         def is_mode(at, what):
-            return pick([int(m[at] == what) for m in modes], j) == 1
-        load_n = pick(LOAD, j)
-        is_h = (first == 1) & (second == 0)
-        before = lax.max(j - 1, 0)
-        own_h_before = pick([int(a[4] and not a[5] and a[0] < N1) for a in JOBS], before)
+            return this["after" if at else "before"] == ("-srhv" if at else "kzlhv").index(what)
 
         for at, tiles in AHEAD.items():
-            @pl.when(j == at)
+            @once(j == at)
             def _():
                 for t in tiles:
                     send_across(t)
-        @pl.when(j == 2)
+        @once(j == 2)
         def _():
             for q in range(M // C):
                 tokens(q).wait_recv()
-        @pl.when(j == 6)
+        @once(j == 6)
         def _():
             for q in range(M // C, own_rows // C):
                 tokens(q).wait_recv()
-        @pl.when(j == TURN)
+        @once(j == TURN)
         def _():
             turn().wait_recv()
             for p, (row, _) in enumerate(PIECES):
                 if row >= TURN_ROW:
                     late_send(p).start()
         for at, ps in SPREAD.items():
-            @pl.when(j == at)
+            @once(j == at)
             def _():
                 for p in ps:
                     late_send(p).wait_recv()
                 for p in ps:
                     late_across(p).start()
 
-        new = pick(NEW, j) == 1
-        @pl.when(j == 2)
+        new = this["new"] == 1
+        @once(j == 2)
         def _():
             start_x(rows, slot_x)
 
@@ -381,17 +371,17 @@
         def _():
             start_x(load_n, 1 - slot_x)
 
-        @pl.when(j == 2)
-        def _():
-            start_x(pick([JOBS[4][0]], j), 1 - slot_x)
-
-        @pl.when(is_mode(0, "z"))
+        @once(j == 2)
+        def _():
+            start_x(jnp.int32(JOBS[4][0]), 1 - slot_x)
+
+        @once(is_mode(0, "z"))
         def _():
             @pl.loop(0, M // R)
             def _(r):
                 acc[pl.ds(pl.multiple_of(r * R, R), R)] = jnp.zeros((R, acc.shape[1]), f32)
 
-        @pl.when(is_mode(0, "l"))
+        @once(is_mode(0, "l"))
         def _():
             swap(rows, False).start()
             swap(rows, False).wait()
@@ -408,21 +398,21 @@
                 at = pl.ds(pl.multiple_of(r * R, R), R)
                 acc[at] = xv[slot, at].astype(f32)
 
-        @pl.when(j == FETCH)
+        @once(j == FETCH)
         def _():
             pltpu.make_async_copy(sh, xv.at[1], x_load.at[1]).start()
 
-        @pl.when(is_mode(0, "h"))
+        @once(is_mode(0, "h"))
         def _():
             pltpu.make_async_copy(sh, xv.at[1], x_load.at[1]).wait()
             from_rows(1)
 
-        @pl.when(is_mode(0, "v"))
+        @once(is_mode(0, "v"))
         def _():
             from_rows(0)
 
         for k, at_job in enumerate(FINAL):
-            @pl.when(j == at_job)
+            @once(j == at_job)
             def _():
                 for q in range(M // C):
                     products(k, q).wait_recv()
@@ -457,7 +447,7 @@
 
             half_h = (src == LATE) & (f == NF - 1)
 
-            @pl.when((first == 0) & jnp.logical_not(half_h))
+            @pl.when((first == 0) & (second == 1) & jnp.logical_not(half_h))
             def _():
                 load_h(slot, rows, f, YS).wait()
 
@@ -465,12 +455,10 @@
             def _():
                 load_h(slot, rows, f, YS, True).wait()
 
-            def load_next():
-                prefetch(1 - slot, jnp.where(ends, rows_n, rows), jnp.where(ends, src_n, src), jnp.where(ends, f0_n, f + 1),
-                         jnp.where(ends, first_n, first), jnp.where(ends, second_n, second), jnp.where(ends, fresh_n, fresh))
-
-            patient = (j >= PATIENT[0]) & (j <= PATIENT[-1])
-            pl.when(jnp.logical_not(patient | (ends & (j == NJ - 1))))(load_next)
+            @pl.when(jnp.logical_not(ends & (j == NJ - 1)))
+            def _():
+                prefetch(1 - slot, *[jnp.where(ends, nxt[k], f + 1 if k == "f0" else this[k])
+                                     for k in ("rows", "src", "f0", "first", "second", "fresh")])
 
             @pl.when(first == 1)
             def _():
@@ -488,8 +476,6 @@
                     cols = slice(c, c + NC)
                     acc[:, cols] += jnp.dot(hv[slot], dv[slot, :, cols], preferred_element_type=f32)
 
-            pl.when(patient)(load_next)
-
             @pl.when(is_h & (rows < N1))
             def _():
                 store_h(slot, rows, f)[0].start()
@@ -506,34 +492,34 @@
             store_h((step0 + n - 1) % 2, rows, f0)[1].wait()
 
         for at, pairs in SENDS.items():
-            @pl.when(j == at)
+            @once(j == at)
             def _():
                 for k, t in pairs:
                     hidden(k, t, t == NF - 1).start()
 
         for at, ps in FORWARD.items():
-            @pl.when(j == at)
+            @once(j == at)
             def _():
                 for p in ps:
                     late_send(p).start()
 
-        @pl.when(is_mode(1, "s"))
+        @once(is_mode(1, "s"))
         def _():
             swap(rows, True).start()
             swap(rows, True).wait()
 
-        @pl.when(is_mode(1, "h"))
+        @once(is_mode(1, "h"))
         def _():
             to_rows(slot_x)
             copy = pltpu.make_async_copy(xv.at[slot_x], sh, s_sem)
             copy.start()
             copy.wait()
 
-        @pl.when(is_mode(1, "v"))
+        @once(is_mode(1, "v"))
         def _():
             to_rows(0)
 
-        @pl.when(is_mode(1, "r"))
+        @once(is_mode(1, "r"))
         def _():
             for q in range(M // C):
                 @pl.loop(0, C // R)
@@ -545,7 +531,7 @@
                 store(rows - 2, q, slot_x).wait()
                 products(rows - 2, q).start()
 
-        @pl.when(j == LEAVE)
+        @once(j == LEAVE)
         def _():
             @pl.loop(0, M // R)
             def _(r):
@@ -553,9 +539,9 @@
                     buf, k, row = spot(b, gv, uv)
                     at = pl.ds(pl.multiple_of(r * R, R), R)
                     buf[k, pl.ds(pl.multiple_of(row + r * R, R), R)] = acc[at, b * FT:(b + 1) * FT].astype(bf16)
-        return step0 + n
-
-    lax.fori_loop(0, NJ, job, jnp.int32(0))
+        return step0 + n, word_n, (is_h & (rows < N1)).astype(jnp.int32)
+
+    lax.fori_loop(0, NJ, job, (jnp.int32(0), jnp.int32(words[0]), jnp.int32(0)))
 
     for q in range(own_rows // C):
         tokens(q).wait_send()

time: 1280 us -> 1280 us (level)
  no operation moved by 1% of the time
where the time goes in v5:
time: 1280 us
  Pallas kernels  1280 us (100%)
    pallas_call x1, Pallas kernels, body(): pl.pallas_call(kernel, out_shape=[pltpu.VMEM((2, d, FT), bf)] * 2 + [pltp...  1270 us

profile of v5, /device:TPU:0, one launch (start us, length us, event | category | flops | bytes accessed | tf_op | source)
XLA Modules:
  0.0 1278.1 jit_solution(4529951446400873758)
XLA Ops:
  0.0 1270.8 %shard_map.46 = (bf16[2,5120,256]{2,1,0:T(8,128)(2,1)S(1)}, bf16[2,5120,256]{2,1,0:T(8,128)(2,1)S(1)}, f32[1024,5120]{1,0:T(8,128)S(1)}, bf16[2,1024,5120]{2,1,0...) custom-call(bf16[2048,5120]{1,0:T(8,128)(2,1)} %x.1, ...), custom_call_target="tpu_custom_call" | custom-call | tf_op jit(solution)/shard_map/pallas_call | solution.py:602
  1270.8 7.3 shard_map.47

commit v6 on v4

--- a/solution.py
+++ b/solution.py
@@ -20,55 +20,17 @@
 
 O1, O2, N1, N2 = range(4)
 MINE, YS, LATE = range(3)
-JOBS = (
-    (O1, MINE, 0, 14, 1, 1, "zs"),
-    (O2, MINE, 0, 14, 1, 1, "zs"),
-    (N1, MINE, 0, 14, 1, 1, "z-"),
-    (N1, YS, 0, 5, 1, 1, "k-"),
-    (O1, YS, 0, 5, 1, 0, "k-"),
-    (O2, YS, 0, 5, 1, 0, "k-"),
-    (N1, YS, 5, 1, 1, 1, "kr"),
-    (N2, MINE, 0, 14, 1, 1, "z-"),
-    (N2, YS, 0, 7, 1, 1, "k-"),
-    (N1, YS, 6, 2, 1, 0, "k-"),
-    (O1, YS, 5, 3, 1, 0, "k-"),
-    (O2, YS, 5, 3, 1, 0, "k-"),
-    (N2, YS, 7, 2, 1, 1, "kr"),
-    (O1, YS, 0, 8, 0, 1, "ls"),
-    (O2, YS, 0, 8, 0, 1, "ls"),
-    (N1, YS, 8, 2, 1, 0, "k-"),
-    (N2, YS, 9, 1, 1, 0, "k-"),
-    (O1, YS, 8, 2, 1, 0, "k-"),
-    (O2, YS, 8, 2, 1, 0, "k-"),
-    (N1, YS, 10, 1, 1, 0, "k-"),
-    (O1, YS, 10, 1, 1, 0, "k-"),
-    (O2, YS, 10, 1, 1, 0, "k-"),
-    (N2, YS, 10, 1, 1, 0, "k-"),
-    (O1, YS, 8, 3, 0, 1, "l-"),
-    (O1, LATE, 6, 2, 0, 1, "ks"),
-    (N1, YS, 11, 1, 1, 0, "k-"),
-    (O1, YS, 11, 1, 1, 0, "k-"),
-    (O2, YS, 11, 1, 1, 0, "k-"),
-    (N2, YS, 11, 1, 1, 0, "k-"),
-    (O2, YS, 8, 4, 0, 1, "lh"),
-    (N1, YS, 12, 1, 1, 0, "k-"),
-    (N2, YS, 12, 1, 1, 0, "k-"),
-    (O1, YS, 12, 1, 1, 0, "k-"),
-    (O2, YS, 12, 1, 1, 0, "k-"),
-    (O1, YS, 11, 2, 0, 1, "l-"),
-    (N2, YS, 13, 1, 1, 0, "k-"),
-    (N1, YS, 13, 1, 1, 0, "k-"),
-    (O1, YS, 13, 1, 1, 0, "k-"),
-    (O2, YS, 13, 1, 1, 0, "k-"),
-    (O1, YS, 13, 1, 0, 1, "k-"),
-    (O1, LATE, 8, 2, 0, 1, "k-"),
-    (O1, LATE, 10, 2, 0, 1, "kv"),
-    (O2, YS, 12, 2, 0, 1, "h-"),
-    (O2, LATE, 9, 3, 0, 1, "k-"),
-    (O2, LATE, 12, 1, 0, 1, "k-"),
-    (O2, LATE, 13, 1, 0, 1, "k-"),
-    (O1, LATE, 12, 2, 0, 1, "v-"),
+ORDER = (
+    "O1M0014Bzs", "O2M0014Bzs", "N1M0014Bz-", "N1Y0005Bk-", "O1Y0005Fk-", "O2Y0005Fk-", "N1Y0501Bkr",
+    "N2M0014Bz-", "N2Y0007Bk-", "N1Y0602Fk-", "O1Y0503Fk-", "O2Y0503Fk-", "N2Y0702Bkr", "O1Y0008Sls",
+    "O2Y0008Sls", "N1Y0802Fk-", "N2Y0901Fk-", "O1Y0802Fk-", "O2Y0802Fk-", "N1Y1001Fk-", "O1Y1001Fk-",
+    "O2Y1001Fk-", "N2Y1001Fk-", "O1Y0803Sl-", "O1L0602Sks", "N1Y1101Fk-", "O1Y1101Fk-", "O2Y1101Fk-",
+    "N2Y1101Fk-", "O2Y0804Slh", "N1Y1201Fk-", "N2Y1201Fk-", "O1Y1201Fk-", "O2Y1201Fk-", "O1Y1102Sl-",
+    "N2Y1301Fk-", "N1Y1301Fk-", "O1Y1301Fk-", "O2Y1301Fk-", "O1Y1301Sk-", "O1L0802Sk-", "O1L1002Skv",
+    "O2Y1202Sh-", "O2L0903Sk-", "O2L1201Sk-", "O2L1301Sk-", "O1-0001Nk-", "O1L1202Sv-",
 )
+JOBS = tuple((("O1", "O2", "N1", "N2").index(o[:2]), "MYL-".index(o[2]), int(o[3:5]), int(o[5:7]), int(o[7] in "BF"), int(o[7] in "BS"), o[8:])
+             for o in ORDER)
 NJ = len(JOBS)
 AHEAD = {2: (0, 1), 3: (2, 3), 8: (6,)}
 FORWARD = {9: (0, 1), 15: (2, 3), 19: (4,)}
@@ -79,7 +41,6 @@
 FINAL = (23, 29)
 FETCH = 39
 LEAVE = 45
-PATIENT = (43, 44, 45)
 SECOND = 12
 
 
@@ -105,6 +66,24 @@
 
 
 SLOT, NEW, LOAD, FRESH = plan()
+FIELDS = (("rows", 4), ("src", 4), ("f0", 16), ("n", 16), ("first", 2), ("second", 2), ("slot", 2), ("new", 2), ("load", 8),
+          ("fresh", 16), ("before", 8), ("after", 8))
+
+
+def packed(j):
+    rows, src, f0, n, first, second, (before, after) = JOBS[j]
+    values = (rows, src, f0, n, first, second, SLOT[j], NEW[j], LOAD[j] + 1, FRESH[j], "kzlhv".index(before), "-srhv".index(after))
+    word, scale = 0, 1
+    for value, (_, size) in zip(values, FIELDS):
+        word, scale = word + value * scale, scale * size
+    return word
+
+
+def unpack(word):
+    got = {}
+    for name, size in FIELDS:
+        got[name], word = lax.rem(word, size), lax.div(word, size)
+    return got
 
 
 def spot(b, gv, uv):
@@ -324,22 +303,19 @@
     start_x(jnp.int32(O1), 0)
     prefetch(0, jnp.int32(O1), jnp.int32(MINE), jnp.int32(0), jnp.int32(1), jnp.int32(1), jnp.int32(NF))
 
-    columns = [[job[i] for job in JOBS] for i in range(6)]
-    modes = [job[6] for job in JOBS]
-
-    def job(j, step0):
-        rows, src, f0, n, first, second = [pick(c, j) for c in columns]
-        after = lax.min(j + 1, NJ - 1)
-        rows_n, src_n, f0_n, _, first_n, second_n = [pick(c, after) for c in columns]
-        fresh, fresh_n = pick(FRESH, j), pick(FRESH, after)
-        slot_x = pick(SLOT, j)
+    words = [packed(j) for j in range(NJ)]
+
+    def job(j, carry):
+        step0, word, own_h_before = carry
+        this = unpack(word)
+        rows, src, f0, n, first, second = (this[k] for k in ("rows", "src", "f0", "n", "first", "second"))
+        word_n = pick(words[1:] + words[-1:], j)
+        nxt = unpack(word_n)
+        fresh, slot_x, load_n = this["fresh"], this["slot"], this["load"] - 1
+        is_h = (first == 1) & (second == 0)
 
         def is_mode(at, what):
-            return pick([int(m[at] == what) for m in modes], j) == 1
-        load_n = pick(LOAD, j)
-        is_h = (first == 1) & (second == 0)
-        before = lax.max(j - 1, 0)
-        own_h_before = pick([int(a[4] and not a[5] and a[0] < N1) for a in JOBS], before)
+            return this["after" if at else "before"] == ("-srhv" if at else "kzlhv").index(what)
 
         for at, tiles in AHEAD.items():
             @pl.when(j == at)
@@ -368,7 +344,7 @@
                 for p in ps:
                     late_across(p).start()
 
-        new = pick(NEW, j) == 1
+        new = this["new"] == 1
         @pl.when(j == 2)
         def _():
             start_x(rows, slot_x)
@@ -383,7 +359,7 @@
 
         @pl.when(j == 2)
         def _():
-            start_x(pick([JOBS[4][0]], j), 1 - slot_x)
+            start_x(jnp.int32(JOBS[4][0]), 1 - slot_x)
 
         @pl.when(is_mode(0, "z"))
         def _():
@@ -457,7 +433,7 @@
 
             half_h = (src == LATE) & (f == NF - 1)
 
-            @pl.when((first == 0) & jnp.logical_not(half_h))
+            @pl.when((first == 0) & (second == 1) & jnp.logical_not(half_h))
             def _():
                 load_h(slot, rows, f, YS).wait()
 
@@ -465,12 +441,10 @@
             def _():
                 load_h(slot, rows, f, YS, True).wait()
 
-            def load_next():
-                prefetch(1 - slot, jnp.where(ends, rows_n, rows), jnp.where(ends, src_n, src), jnp.where(ends, f0_n, f + 1),
-                         jnp.where(ends, first_n, first), jnp.where(ends, second_n, second), jnp.where(ends, fresh_n, fresh))
-
-            patient = (j >= PATIENT[0]) & (j <= PATIENT[-1])
-            pl.when(jnp.logical_not(patient | (ends & (j == NJ - 1))))(load_next)
+            @pl.when(jnp.logical_not(ends & (j == NJ - 1)))
+            def _():
+                prefetch(1 - slot, *[jnp.where(ends, nxt[k], f + 1 if k == "f0" else this[k])
+                                     for k in ("rows", "src", "f0", "first", "second", "fresh")])
 
             @pl.when(first == 1)
             def _():
@@ -487,8 +461,6 @@
                 for c in range(0, acc.shape[1], NC):
                     cols = slice(c, c + NC)
                     acc[:, cols] += jnp.dot(hv[slot], dv[slot, :, cols], preferred_element_type=f32)
-
-            pl.when(patient)(load_next)
 
             @pl.when(is_h & (rows < N1))
             def _():
@@ -553,9 +525,9 @@
                     buf, k, row = spot(b, gv, uv)
                     at = pl.ds(pl.multiple_of(r * R, R), R)
                     buf[k, pl.ds(pl.multiple_of(row + r * R, R), R)] = acc[at, b * FT:(b + 1) * FT].astype(bf16)
-        return step0 + n
-
-    lax.fori_loop(0, NJ, job, jnp.int32(0))
+        return step0 + n, word_n, (is_h & (rows < N1)).astype(jnp.int32)
+
+    lax.fori_loop(0, NJ, job, (jnp.int32(0), jnp.int32(words[0]), jnp.int32(0)))
 
     for q in range(own_rows // C):
         tokens(q).wait_send()

time: 1280 us -> 1280 us (level)
  no operation moved by 1% of the time
where the time goes in v6:
time: 1280 us
  Pallas kernels  1280 us (100%)
    pallas_call x1, Pallas kernels, body(): pl.pallas_call(kernel, out_shape=[pltpu.VMEM((2, d, FT), bf)] * 2 + [pltp...  1270 us

profile of v6, /device:TPU:0, one launch (start us, length us, event | category | flops | bytes accessed | tf_op | source)
XLA Modules:
  0.0 1281.1 jit_solution(13254224135792288965)
XLA Ops:
  0.0 1273.7 %shard_map.46 = (bf16[2,5120,256]{2,1,0:T(8,128)(2,1)S(1)}, bf16[2,5120,256]{2,1,0:T(8,128)(2,1)S(1)}, f32[1024,5120]{1,0:T(8,128)S(1)}, bf16[2,1024,5120]{2,1,0...) custom-call(bf16[2048,5120]{1,0:T(8,128)(2,1)} %x.1, ...), custom_call_target="tpu_custom_call" | custom-call | tf_op jit(solution)/shard_map/pallas_call | solution.py:588
  1273.7 7.3 shard_map.47

commit v7 on v5

--- a/solution.py
+++ b/solution.py
@@ -9,14 +9,14 @@
 M = 1024
 FT = 256
 NF = 14
-C = 256
+C = 512
 WC = 384
 NC = 1280
 MS = 512
 R = 32
 L0 = 6
 TURN_ROW = 2688
-PIECES = ((1536, 256), (1792, 256), (2048, 256), (2304, 256), (2560, 128), (2688, 128), (2816, 256), (3072, 256), (3328, 128))
+PIECES = ((1536, 512), (2048, 512), (2560, 128), (2688, 128), (2816, 256), (3072, 256), (3328, 128))
 
 O1, O2, N1, N2 = range(4)
 MINE, YS, LATE = range(3)
@@ -33,11 +33,11 @@
              for o in ORDER)
 NJ = len(JOBS)
 AHEAD = {2: (0, 1), 3: (2, 3), 8: (6,)}
-FORWARD = {9: (0, 1), 15: (2, 3), 19: (4,)}
-SENDS = {9: ((0, 6), (0, 7)), 15: ((0, 8), (0, 9)), 16: ((1, 9),), 19: ((0, 10),), 25: ((0, 11),), 28: ((1, 10), (1, 11)),
-         31: ((1, 12),), 35: ((1, 13),), 36: ((0, 12), (0, 13))}
+FORWARD = {9: (0,), 15: (1,), 19: (2,)}
+SENDS = {9: ((0, 6, 2),), 15: ((0, 8, 2),), 16: ((1, 9, 1),), 19: ((0, 10, 1),), 25: ((0, 11, 1),), 28: ((1, 10, 2),),
+         31: ((1, 12, 1),), 35: ((1, 13, 1),), 36: ((0, 12, 1), (0, 13, 1))}
 TURN = 8
-SPREAD = {17: (0, 1), 35: (2, 3), 40: (4, 5, 6), 43: (7,), 44: (8,)}
+SPREAD = {17: (0,), 35: (1,), 40: (2, 3, 4), 43: (5,), 44: (6,)}
 FINAL = (23, 29)
 FETCH = 39
 LEAVE = 45
@@ -103,7 +103,6 @@
     dc = wd.shape[1]
     f32, bf16 = jnp.float32, jnp.bfloat16
     last = (NF - 1) * FT
-    own_rows = x.shape[0]
 
     barrier = pltpu.get_barrier_semaphore()
     for who in (to_x, to_y, to_core):
@@ -127,8 +126,8 @@
     def col(t):
         return t * FT if isinstance(t, int) else pl.multiple_of(t * FT, FT)
 
-    def tokens(q):
-        return remote(x.at[pl.ds(q * C, C)], gn.at[q // (M // C), pl.ds(q % (M // C) * C, C)], n_send.at[q], n_recv.at[q], to_x)
+    def tokens(k):
+        return remote(x.at[pl.ds(k * M, M)], gn.at[k], n_send.at[k], n_recv.at[k], to_x)
 
     def mine(k, c):
         at = c * WC if isinstance(c, int) else pl.multiple_of(c * WC, WC)
@@ -167,16 +166,16 @@
     def turn():
         return remote(wd.at[pl.ds(TURN_ROW, ff - TURN_ROW)], xd, t_sem.at[0], t_sem.at[1], to_x)
 
-    def hidden(k, t, end=False):
-        at = (k, t, slice(None), pl.ds(NF * FT - ff, ff - last)) if end else (k, t)
+    def hidden(k, t, n):
+        at = (k, t, slice(None), pl.ds(NF * FT - ff, ff - last)) if t == NF - 1 else (k, pl.ds(t, n))
         return remote(hs.at[at], hr.at[at], h_send.at[k, t], h_recv.at[k, t], to_x)
 
     def products(k, q):
         rows = pl.ds(q * C, C)
         return remote(prod.at[k, rows], part.at[k, rows], r_send.at[k, q], r_recv.at[k, q], to_x)
 
-    for q in range(own_rows // C):
-        tokens(q).start()
+    for k in range(2):
+        tokens(k).start()
     turn().start()
     for t in range(NF):
         for k in range(3):
@@ -285,14 +284,17 @@
 
         @once(src == LATE)
         def _():
+            for k, t, n in (g for groups in SENDS.values() for g in groups):
+                @pl.when((rows == k) & (f == t))
+                def _():
+                    hidden(k, t, n).wait_recv()
+
             @pl.when(f < NF - 1)
             def _():
-                hidden(rows, f).wait_recv()
                 load_h(slot, rows, f, LATE).start()
 
             @pl.when(f == NF - 1)
             def _():
-                hidden(rows, NF - 1, True).wait_recv()
                 hv[slot, :, pl.ds(0, NF * FT - ff)] = jnp.zeros((M, NF * FT - ff), bf16)
                 load_h(slot, rows, NF - 1, LATE, True).start()
             for t in range(L0, NF):
@@ -338,12 +340,10 @@
                     send_across(t)
         @once(j == 2)
         def _():
-            for q in range(M // C):
-                tokens(q).wait_recv()
+            tokens(0).wait_recv()
         @once(j == 6)
         def _():
-            for q in range(M // C, own_rows // C):
-                tokens(q).wait_recv()
+            tokens(1).wait_recv()
         @once(j == TURN)
         def _():
             turn().wait_recv()
@@ -494,8 +494,8 @@
         for at, pairs in SENDS.items():
             @once(j == at)
             def _():
-                for k, t in pairs:
-                    hidden(k, t, t == NF - 1).start()
+                for k, t, n in pairs:
+                    hidden(k, t, n).start()
 
         for at, ps in FORWARD.items():
             @once(j == at)
@@ -543,8 +543,8 @@
 
     lax.fori_loop(0, NJ, job, (jnp.int32(0), jnp.int32(words[0]), jnp.int32(0)))
 
-    for q in range(own_rows // C):
-        tokens(q).wait_send()
+    for k in range(2):
+        tokens(k).wait_send()
     turn().wait_send()
     for t in range(NF):
         for k in range(3):
@@ -560,8 +560,8 @@
         for q in range(M // C):
             products(k, q).wait_send()
     for pairs in SENDS.values():
-        for k, t in pairs:
-            hidden(k, t, t == NF - 1).wait_send()
+        for k, t, n in pairs:
+            hidden(k, t, n).wait_send()
 
 
 def write(gv, uv, acc, out, yv, sem):
@@ -596,7 +596,7 @@
         shapes = [(2, M, d), (kd, ff), (kd, ff), (ff, dc), (2, kd, ff), (2, kd, ff), (2, ff, dc),
                   (2, ff - L0 * FT, dc), (ff - TURN_ROW, dc), nh, nh, nh]
         dma = pltpu.SemaphoreType.DMA
-        nl, nn, nw = len(PIECES), r // C, ff // WC
+        nl, nn, nw = len(PIECES), r // M, ff // WC
         work = [jax.ShapeDtypeStruct(s, bf) for s in shapes] + [
             jax.ShapeDtypeStruct((2, M, d), f32), jax.ShapeDtypeStruct((M, d), bf), jax.ShapeDtypeStruct((2, M, d), bf), jax.ShapeDtypeStruct((2, M, d), bf)]
         gv, uv, acc, *_ = pl.pallas_call(

time: 1280 us -> 1280 us (level)
  no operation moved by 1% of the time
where the time goes in v7:
time: 1280 us
  Pallas kernels  1280 us (100%)
    pallas_call x1, Pallas kernels, body(): pl.pallas_call(kernel, out_shape=[pltpu.VMEM((2, d, FT), bf)] * 2 + [pltp...  1270 us

profile of v7, /device:TPU:0, one launch (start us, length us, event | category | flops | bytes accessed | tf_op | source)
XLA Modules:
  0.0 1278.8 jit_solution(6550881710515935069)
XLA Ops:
  0.0 1271.5 %shard_map.46 = (bf16[2,5120,256]{2,1,0:T(8,128)(2,1)S(1)}, bf16[2,5120,256]{2,1,0:T(8,128)(2,1)S(1)}, f32[1024,5120]{1,0:T(8,128)S(1)}, bf16[2,1024,5120]{2,1,0...) custom-call(bf16[2048,5120]{1,0:T(8,128)(2,1)} %x.1, ...), custom_call_target="tpu_custom_call" | custom-call | tf_op jit(solution)/shard_map/pallas_call | solution.py:602
  1271.5 7.3 shard_map.47

commit v8 on v5

--- a/solution.py
+++ b/solution.py
@@ -22,7 +22,7 @@
 MINE, YS, LATE = range(3)
 ORDER = (
     "O1M0014Bzs", "O2M0014Bzs", "N1M0014Bz-", "N1Y0005Bk-", "O1Y0005Fk-", "O2Y0005Fk-", "N1Y0501Bkr",
-    "N2M0014Bz-", "N2Y0007Bk-", "N1Y0602Fk-", "O1Y0503Fk-", "O2Y0503Fk-", "N2Y0702Bkr", "O1Y0008Sls",
+    "N2M0014Bz-", "N2Y0007Bk-", "N1Y0602Fk-", "N2Y0702Bkr", "O1Y0503Fk-", "O2Y0503Fk-", "O1Y0008Sls",
     "O2Y0008Sls", "N1Y0802Fk-", "N2Y0901Fk-", "O1Y0802Fk-", "O2Y0802Fk-", "N1Y1001Fk-", "O1Y1001Fk-",
     "O2Y1001Fk-", "N2Y1001Fk-", "O1Y0803Sl-", "O1L0602Sks", "N1Y1101Fk-", "O1Y1101Fk-", "O2Y1101Fk-",
     "N2Y1101Fk-", "O2Y0804Slh", "N1Y1201Fk-", "N2Y1201Fk-", "O1Y1201Fk-", "O2Y1201Fk-", "O1Y1102Sl-",

time: 1280 us -> 1280 us (level)
  no operation moved by 1% of the time
where the time goes in v8:
time: 1280 us
  Pallas kernels  1280 us (100%)
    pallas_call x1, Pallas kernels, body(): pl.pallas_call(kernel, out_shape=[pltpu.VMEM((2, d, FT), bf)] * 2 + [pltp...  1270 us

profile of v8, /device:TPU:0, one launch (start us, length us, event | category | flops | bytes accessed | tf_op | source)
XLA Modules:
  0.0 1278.1 jit_solution(10699614226637643173)
XLA Ops:
  0.0 1270.8 %shard_map.46 = (bf16[2,5120,256]{2,1,0:T(8,128)(2,1)S(1)}, bf16[2,5120,256]{2,1,0:T(8,128)(2,1)S(1)}, f32[1024,5120]{1,0:T(8,128)S(1)}, bf16[2,1024,5120]{2,1,0...) custom-call(bf16[2048,5120]{1,0:T(8,128)(2,1)} %x.1, ...), custom_call_target="tpu_custom_call" | custom-call | tf_op jit(solution)/shard_map/pallas_call | solution.py:602
  1270.8 7.3 shard_map.47
